TPU v7x, 16 devices: a 4x2x1 block of a 4x4x8 slice. The times are simulated.
16 devices in a mesh: data: 2 (over y, z), tp: 8 (over x, core).
Axes of the slice: x: 4, y: 2, z: 1, core: 2. Of those that a mesh axis runs over, the one named last changes fastest.
The devices are a block of a 4x4x8 slice.
Arguments:
- x_tokens: bfloat16 [8192, 4096], P(('data', 'tp')), parts along dimension 0
- ln_gamma: float32 [4096], replicated
- w_qkv: bfloat16 [4096, 32, 384], P(None, 'tp')
- w_out: bfloat16 [32, 128, 4096], P('tp')
- w_up: bfloat16 [4096, 11008], P(None, 'tp')
- w_down: bfloat16 [11008, 4096], P('tp')
Outputs:
- output: bfloat16 [8192, 4096], P(('data', 'tp')), parts along dimension 0
There are 2 independent parts. A program takes and returns all parts, laid end to end along the dimension named above; an argument that names none is the same for every part.
All inputs are finite; a program needn't handle non-finite values.
Results may differ from a plain program's by a relative error of at most 0.00288605.
Values are sent between devices in bfloat16 or wider.
A program may use at most 768 MiB of HBM per device.

v0:
```python
import math
import jax
import jax.numpy as jnp
from jax import lax
from jax.sharding import PartitionSpec as P

LN_EPS = 1e-6


def layer_norm(row_vals, ln_gain):
    row_mean = jnp.mean(row_vals, axis=-1, keepdims=True)
    centered = row_vals - row_mean
    row_var = jnp.mean(centered * centered, axis=-1, keepdims=True)
    return (centered * lax.rsqrt(row_var + LN_EPS) * ln_gain).astype(jnp.bfloat16)


def block_rows(row_count, head_count):
    return min(row_count, 2 ** int(math.log2(max(8, 4096 // head_count))))


def attend(query_rows, key_rows, value_rows):
    row_count, head_count, head_dim = query_rows.shape
    q_size = block_rows(row_count, head_count)
    attn_scale = head_dim ** -0.5

    def one_block(query_blk):
        scores = jnp.einsum("qhe,khe->hqk", query_blk, key_rows, preferred_element_type=jnp.float32) * attn_scale
        row_max = jnp.max(scores, axis=-1, keepdims=True)
        exp_scores = jnp.exp(scores - row_max)
        exp_sum = jnp.sum(exp_scores, axis=-1, keepdims=True)
        block_out = jnp.einsum("hqk,khe->hqe", exp_scores.astype(jnp.bfloat16), value_rows, preferred_element_type=jnp.float32)
        return (block_out / exp_sum).astype(jnp.bfloat16)

    return lax.map(one_block, query_rows.reshape(row_count // q_size, q_size, head_count, head_dim))


def solution(mesh):
    def local_block(x_loc, ln_gamma, w_qkv, w_out, w_up, w_down):
        model_dim = x_loc.shape[1]
        head_dim = w_qkv.shape[2] // 3
        residual = x_loc.astype(jnp.float32)
        normed = layer_norm(residual, ln_gamma)
        gathered = lax.all_gather(normed, "tp", axis=0, tiled=True)
        seq_len = gathered.shape[0]
        qkv_rows = jnp.einsum("sd,dhc->shc", gathered, w_qkv, preferred_element_type=jnp.float32).astype(jnp.bfloat16)
        head_out = attend(qkv_rows[:, :, :head_dim], qkv_rows[:, :, head_dim:2 * head_dim], qkv_rows[:, :, 2 * head_dim:])
        attn_part = jnp.einsum("nhqe,hed->nqd", head_out, w_out, preferred_element_type=jnp.float32).reshape(seq_len, model_dim)
        pre_act = jnp.dot(gathered, w_up, preferred_element_type=jnp.float32)
        hidden = jax.nn.gelu(pre_act, approximate=True).astype(jnp.bfloat16)
        part_sum = attn_part + jnp.dot(hidden, w_down, preferred_element_type=jnp.float32)
        reduced = lax.psum_scatter(part_sum, "tp", scatter_dimension=0, tiled=True)
        return (residual + reduced).astype(jnp.bfloat16)

    row_spec = P(("data", "tp"), None)
    return jax.shard_map(local_block, mesh=mesh, in_specs=(row_spec, P(None), P(None, "tp", None), P("tp", None, None), P(None, "tp"), P("tp", None)), out_specs=row_spec, check_vma=False)
```

profile of v0, /device:TPU:112, one launch (start us, length us, event | category | flops | bytes accessed | tf_op | source)
XLA Modules:
  0.0 1023.3 jit_solution(45788662130904930)
XLA Ops:
  6.5 0.0 all-gather.2.cloned.1.call-start
  6.6 0.0 copy-start
  6.6 3.0 convert_reduce_fusion
  9.5 3.4 fusion.40
  12.9 0.0 copy-done
  13.0 5.0 fusion.42
  18.0 0.1 all-gather.2.cloned.1.call-update
  18.0 0.1 reduce-scatter.2.cloned.1.call-start
  18.1 155.6 %all-gather.2.cloned.1.call-done = bf16[4096,4096]{1,0:T(8,128)(2,1)} async-done(((bf16[512,4096]{1,0:T(8,128)(2,1)}), bf16[4096,4096]{1,0:T(8,128)(2,1)}) %all-gather.2.cloned.1.call-update) | async-done | bytes 33554448 | tf_op jit(solution)/shard_map/all_gather | solution.py:43
  173.7 59.1 %fusion.35 = bf16[4096,4,384]{2,0,1:T(8,128)(2,1)S(1)} fusion(bf16[4096,4,384]{2,1,0:T(4,128)(2,1)} %param.10, bf16[4096,4096]{1,0:T(8,128)(2,1)} %all-gather.2.cloned.1.call-done), kind=kOutput, calls=%fused_computation.35 | convolution fusion | flops 51545899008 | bytes 58720256 | tf_op jit(solution)/shard_map/sd,dhc->shc/dot_general | solution.py:45
  232.9 4.9 fusion.50
  237.8 293.7 %while.10 = (s32[]{:T(128)}, bf16[4,4,1024,128]{3,2,1,0:T(8,128)(2,1)}, bf16[4,1024,4,128]{3,1,0,2:T(8,128)(2,1)}, bf16[4096,4,128]{2,0,1:T(8,128)(2,1)}, bf16[4096,4,128]{2,0,1:T(8,128)(2,1)}, /*index=5*/s32[]{:T(128)}) while((s32[]{:T(128)}, bf16[4,4,1024,128]{3,2,1,0:T(8,128)(2,1)}, bf16[4,1024,4,128]{3,1,0,2:T(8,128)(2,1)}, ...), condition=%wide.region_5.6_spmd, body=%wide.region_2.5_spmd.sunk | while | flops 8725192704 | bytes 211894352 | solution.py:34
  238.0 26.3 %multiply_reduce_fusion.2 = (f32[4,1024]{1,0:T(4,128)S(1)}, f32[4,1024,4096]{2,1,0:T(8,128)}) fusion(bf16[4096,4,128]{2,0,1:T(8,128)(2,1)} %get-tuple-element.103, bf16[4,1024,4,128]{3,1,0,2:T(8,128)(2,1)} %get-tuple-element.102, s32[]{:T(128)S(6)} %copy.18), kind=kOutput, calls=%fused_computation.1.clone.1 | convolution fusion | flops 4328517632 | bytes 72368128 | tf_op jit(solution)/shard_map/while/body/eval_jaxpr/qhe,khe->hqk/dot_general | solution.py:27
  264.3 21.2 %fusion.69 = f32[4,1024]{1,0:T(4,128)S(1)} fusion(f32[4,1024,4096]{2,1,0:T(8,128)} %get-tuple-element.86, f32[4,1024]{1,0:T(4,128)S(1)} %get-tuple-element.87), kind=kLoop, calls=%fused_computation.2.clone.1 | loop fusion | flops 50327552 | bytes 67141632 | tf_op jit(solution)/shard_map/while/body/eval_jaxpr/reduce_sum | solution.py:30
  285.5 25.8 %fusion.70 = bf16[4,4,1024,128]{3,2,1,0:T(8,128)(2,1)} fusion(bf16[4,4,1024,128]{3,2,1,0:T(8,128)(2,1)} %get-tuple-element.95, s32[]{:T(128)S(6)} %copy.18, bf16[4096,4,128]{2,0,1:T(8,128)(2,1)} %get-tuple-element.104, f32[4,1024,4096]{2,1,0:T(8,128)} %get-tuple-element.86, f32[4,1024]{1,0:T(4,128)S(1)} %get-tuple-element.87, f32[4,1024]{1,0:T(4,128)S(1)} %fusion.69), kind=kOutput, calls=%fused_computation.7.clone.1 | convolution fusion | flops 4346347520 | bytes 72384512 | tf_op jit(solution)/shard_map/while/body/eval_jaxpr/hqk,khe->hqe/dot_general | solution.py:31
  311.3 26.3 %multiply_reduce_fusion.2 = (f32[4,1024]{1,0:T(4,128)S(1)}, f32[4,1024,4096]{2,1,0:T(8,128)}) fusion(bf16[4096,4,128]{2,0,1:T(8,128)(2,1)} %get-tuple-element.103, bf16[4,1024,4,128]{3,1,0,2:T(8,128)(2,1)} %get-tuple-element.102, s32[]{:T(128)S(6)} %copy.18), kind=kOutput, calls=%fused_computation.1.clone.1 | convolution fusion | flops 4328517632 | bytes 72368128 | tf_op jit(solution)/shard_map/while/body/eval_jaxpr/qhe,khe->hqk/dot_general | solution.py:27
  337.6 21.2 %fusion.69 = f32[4,1024]{1,0:T(4,128)S(1)} fusion(f32[4,1024,4096]{2,1,0:T(8,128)} %get-tuple-element.86, f32[4,1024]{1,0:T(4,128)S(1)} %get-tuple-element.87), kind=kLoop, calls=%fused_computation.2.clone.1 | loop fusion | flops 50327552 | bytes 67141632 | tf_op jit(solution)/shard_map/while/body/eval_jaxpr/reduce_sum | solution.py:30
  358.9 25.8 %fusion.70 = bf16[4,4,1024,128]{3,2,1,0:T(8,128)(2,1)} fusion(bf16[4,4,1024,128]{3,2,1,0:T(8,128)(2,1)} %get-tuple-element.95, s32[]{:T(128)S(6)} %copy.18, bf16[4096,4,128]{2,0,1:T(8,128)(2,1)} %get-tuple-element.104, f32[4,1024,4096]{2,1,0:T(8,128)} %get-tuple-element.86, f32[4,1024]{1,0:T(4,128)S(1)} %get-tuple-element.87, f32[4,1024]{1,0:T(4,128)S(1)} %fusion.69), kind=kOutput, calls=%fused_computation.7.clone.1 | convolution fusion | flops 4346347520 | bytes 72384512 | tf_op jit(solution)/shard_map/while/body/eval_jaxpr/hqk,khe->hqe/dot_general | solution.py:31
  384.7 26.3 %multiply_reduce_fusion.2 = (f32[4,1024]{1,0:T(4,128)S(1)}, f32[4,1024,4096]{2,1,0:T(8,128)}) fusion(bf16[4096,4,128]{2,0,1:T(8,128)(2,1)} %get-tuple-element.103, bf16[4,1024,4,128]{3,1,0,2:T(8,128)(2,1)} %get-tuple-element.102, s32[]{:T(128)S(6)} %copy.18), kind=kOutput, calls=%fused_computation.1.clone.1 | convolution fusion | flops 4328517632 | bytes 72368128 | tf_op jit(solution)/shard_map/while/body/eval_jaxpr/qhe,khe->hqk/dot_general | solution.py:27
  411.0 21.2 %fusion.69 = f32[4,1024]{1,0:T(4,128)S(1)} fusion(f32[4,1024,4096]{2,1,0:T(8,128)} %get-tuple-element.86, f32[4,1024]{1,0:T(4,128)S(1)} %get-tuple-element.87), kind=kLoop, calls=%fused_computation.2.clone.1 | loop fusion | flops 50327552 | bytes 67141632 | tf_op jit(solution)/shard_map/while/body/eval_jaxpr/reduce_sum | solution.py:30
  432.3 25.8 %fusion.70 = bf16[4,4,1024,128]{3,2,1,0:T(8,128)(2,1)} fusion(bf16[4,4,1024,128]{3,2,1,0:T(8,128)(2,1)} %get-tuple-element.95, s32[]{:T(128)S(6)} %copy.18, bf16[4096,4,128]{2,0,1:T(8,128)(2,1)} %get-tuple-element.104, f32[4,1024,4096]{2,1,0:T(8,128)} %get-tuple-element.86, f32[4,1024]{1,0:T(4,128)S(1)} %get-tuple-element.87, f32[4,1024]{1,0:T(4,128)S(1)} %fusion.69), kind=kOutput, calls=%fused_computation.7.clone.1 | convolution fusion | flops 4346347520 | bytes 72384512 | tf_op jit(solution)/shard_map/while/body/eval_jaxpr/hqk,khe->hqe/dot_general | solution.py:31
  458.1 26.3 %multiply_reduce_fusion.2 = (f32[4,1024]{1,0:T(4,128)S(1)}, f32[4,1024,4096]{2,1,0:T(8,128)}) fusion(bf16[4096,4,128]{2,0,1:T(8,128)(2,1)} %get-tuple-element.103, bf16[4,1024,4,128]{3,1,0,2:T(8,128)(2,1)} %get-tuple-element.102, s32[]{:T(128)S(6)} %copy.18), kind=kOutput, calls=%fused_computation.1.clone.1 | convolution fusion | flops 4328517632 | bytes 72368128 | tf_op jit(solution)/shard_map/while/body/eval_jaxpr/qhe,khe->hqk/dot_general | solution.py:27
  484.4 21.2 %fusion.69 = f32[4,1024]{1,0:T(4,128)S(1)} fusion(f32[4,1024,4096]{2,1,0:T(8,128)} %get-tuple-element.86, f32[4,1024]{1,0:T(4,128)S(1)} %get-tuple-element.87), kind=kLoop, calls=%fused_computation.2.clone.1 | loop fusion | flops 50327552 | bytes 67141632 | tf_op jit(solution)/shard_map/while/body/eval_jaxpr/reduce_sum | solution.py:30
  505.6 25.8 %fusion.70 = bf16[4,4,1024,128]{3,2,1,0:T(8,128)(2,1)} fusion(bf16[4,4,1024,128]{3,2,1,0:T(8,128)(2,1)} %get-tuple-element.95, s32[]{:T(128)S(6)} %copy.18, bf16[4096,4,128]{2,0,1:T(8,128)(2,1)} %get-tuple-element.104, f32[4,1024,4096]{2,1,0:T(8,128)} %get-tuple-element.86, f32[4,1024]{1,0:T(4,128)S(1)} %get-tuple-element.87, f32[4,1024]{1,0:T(4,128)S(1)} %fusion.69), kind=kOutput, calls=%fused_computation.7.clone.1 | convolution fusion | flops 4346347520 | bytes 72384512 | tf_op jit(solution)/shard_map/while/body/eval_jaxpr/hqk,khe->hqe/dot_general | solution.py:31
  531.5 27.1 %fusion.44 = f32[4,1024,4096,1]{2,1,3,0:T(8,128)} fusion(bf16[4,4,1024,128]{3,2,1,0:T(8,128)(2,1)} %get-tuple-element.32, bf16[4,128,4096]{2,1,0:T(8,128)(2,1)} %param.11), kind=kOutput, calls=%fused_computation.40 | convolution fusion | flops 17179869184 | bytes 75497472 | tf_op jit(solution)/shard_map/nhqe,hed->nqd/dot_general | solution.py:47
  558.5 56.7 %fusion.51 = f32[4096,1376]{0,1:T(8,128)} fusion(bf16[4096,4096]{1,0:T(8,128)(2,1)} %all-gather.2.cloned.1.call-done, bf16[4096,1376]{0,1:T(8,128)(2,1)} %param.12), kind=kOutput, calls=%fused_computation.49 | convolution fusion | flops 46170898432 | bytes 67371008 | tf_op jit(solution)/shard_map/dot_general | solution.py:48
  615.2 67.9 %bitcast_add_fusion = f32[4096,4096]{1,0:T(8,128)} fusion(f32[4,1024,4096,1]{2,1,3,0:T(8,128)} %fusion.44, bf16[1376,4096]{1,0:T(8,128)(2,1)} %param.13, f32[4096,1376]{0,1:T(8,128)} %fusion.51), kind=kOutput, calls=%fused_computation.13 | convolution fusion | flops 46238400512 | bytes 168034304 | tf_op jit(solution)/shard_map/dot_general | solution.py:50
  683.1 0.1 reduce-scatter.2.cloned.1.call-update
  683.2 324.8 %reduce-scatter.2.cloned.1.call-done = f32[512,4096]{1,0:T(8,128)} async-done(((f32[4096,4096]{1,0:T(8,128)}), f32[512,4096]{1,0:T(8,128)}) %reduce-scatter.2.cloned.1.call-update) | async-done | bytes 8388624 | tf_op jit(solution)/shard_map/reduce_scatter | solution.py:51
  1008.0 8.0 fusion.43
  (3 shorter events, 0.0 us)
Async XLA Ops:
  6.5 167.2 %all-gather.2.cloned.1.call-start = ((), (), s32[]{:S(2)}) async-start(), calls=%async_computation.1 | async-start | bytes 37748736 | tf_op jit(solution)/shard_map/all_gather | solution.py:43
  6.6 6.4 copy-start
  18.0 989.9 %reduce-scatter.2.cloned.1.call-start = ((), (), s32[]{:S(2)}) async-start(), calls=%async_computation.2 | async-start | bytes 75497472 | tf_op jit(solution)/shard_map/reduce_scatter | solution.py:51
Sparse Core Ops, SparseCore 0:
  18.2 155.5 all-gather.1
  683.3 324.6 reduce-scatter.1
where the time goes:
time: 1030 us; the launch traced here: 1020 us
  waiting for transfers between devices  481 us (47%)
  matrix products  419 us (41%)
  other arithmetic  104 us (10%)
  between operations  13.9 us (1%)
    reduce_scatter x1, waiting for transfers between devices, local_block(): reduced = lax.psum_scatter(part_sum, 'tp', scatter_dimension=0, tiled=True)  325 us
    all_gather x1, waiting for transfers between devices, local_block(): gathered = lax.all_gather(normed, 'tp', axis=0, tiled=True)  156 us
    dot_general x4, matrix products, one_block(): jnp.einsum('qhe,khe->hqk', query_blk, key_rows, preferred_element_type=jn...  105 us
    dot_general x4, matrix products, one_block(): jnp.einsum('hqk,khe->hqe', exp_scores.astype(jnp.bfloat16), value_rows, p...  103 us
    reduce_sum x4, other arithmetic, one_block(): exp_sum = jnp.sum(exp_scores, axis=-1, keepdims=True)  84.9 us
    dot_general x1, matrix products, local_block(): jnp.dot(hidden, w_down, preferred_element_type=jnp.float32)  67.9 us
    dot_general x1, matrix products, local_block(): jnp.einsum('sd,dhc->shc', gathered, w_qkv, preferred_element_type=jnp.flo...  59.1 us
    dot_general x1, matrix products, local_block(): pre_act = jnp.dot(gathered, w_up, preferred_element_type=jnp.float32)  56.7 us
  transfers between devices with their start and end apart: 2, of which 2 were waited for; matrix products, arithmetic and copies ran while one was open for 0% of the time, Pallas kernels for 0%

commit v1 on v0

v1 whole, which is shorter than its diff:
```python
import functools
import math

import jax
import jax.numpy as jnp
from jax import lax
from jax.experimental import pallas as pl
from jax.experimental.pallas import tpu as pltpu
from jax.sharding import PartitionSpec as P

LN_EPS = 1e-6
MESH = pl.DeviceIdType.MESH
CORES = 2
PIECE = 64
BLOCK = 256
COLS = 512
VMEM_LIMIT = 67_000_000
ANY = pl.BlockSpec(memory_space=pl.ANY)


def norm_kernel(x_ref, g_ref, o_ref):
    vals = x_ref[...].astype(jnp.float32)
    centered = vals - jnp.mean(vals, axis=-1, keepdims=True)
    var = jnp.mean(centered * centered, axis=-1, keepdims=True)
    o_ref[...] = (centered * lax.rsqrt(var + LN_EPS) * g_ref[...]).astype(o_ref.dtype)


def layer_norm(x_loc, ln_gamma):
    rows, width = x_loc.shape
    tile = min(rows, 128)
    return pl.pallas_call(
        norm_kernel,
        grid=(rows // tile,),
        in_specs=[pl.BlockSpec((tile, width), lambda i: (i, 0)), pl.BlockSpec((1, width), lambda i: (0, 0))],
        out_specs=pl.BlockSpec((tile, width), lambda i: (i, 0)),
        out_shape=jax.ShapeDtypeStruct(x_loc.shape, jnp.bfloat16),
        name="norm",
    )(x_loc, ln_gamma.reshape(1, width))


def neighbours(chips):
    me = lax.axis_index("tp")
    chip, core = me // CORES, me % CORES
    right = (chip + 1) % chips * CORES + core
    left = (chip + chips - 1) % chips * CORES + core
    partner = chip * CORES + (1 - core)
    return me, chip, core, right, left, partner


def greet(devices):
    barrier = pltpu.get_barrier_semaphore()
    for device in devices:
        pl.semaphore_signal(barrier, inc=1, device_id={"tp": device}, device_id_type=MESH)
    pl.semaphore_wait(barrier, len(devices))


def remote(src, dst, send_sem, recv_sem, device):
    return pltpu.make_async_remote_copy(
        src_ref=src, dst_ref=dst, send_sem=send_sem, recv_sem=recv_sem, device_id={"tp": device}, device_id_type=MESH
    )


def each(count, body):
    def step(i, carry):
        body(i)
        return carry

    lax.fori_loop(0, count, step, 0)


def gather_kernel(
    chips, x_ref, wq_ref, w1_ref, xg_ref, qkv_ref, h_ref, wq_v, w1_v, lhs, qo, ho,
    w_sem, lhs_sem, qo_sem, ho_sem, send_r, recv_l, send_l, recv_r, send_p, recv_p,
):
    me, chip, core, right, left, partner = neighbours(chips)
    chunk = x_ref.shape[0]
    own_pieces = chunk // PIECE
    half = own_pieces // 2
    arrivals = own_pieces + half
    per_group = BLOCK // PIECE
    own_groups = chunk // BLOCK
    first = own_groups * CORES
    groups = first + arrivals

    greet((right, left, partner))

    load_q = pltpu.make_async_copy(wq_ref, wq_v, w_sem.at[0])
    load_1 = pltpu.make_async_copy(w1_ref, w1_v, w_sem.at[1])

    def own_piece(piece):
        return x_ref.at[pl.ds(pl.multiple_of(piece * PIECE, PIECE), PIECE)]

    def rows_at(device, piece):
        return pl.ds(pl.multiple_of(device * chunk + piece * PIECE, PIECE), PIECE)

    def to_right(j):
        return remote(own_piece(j), xg_ref.at[rows_at(me, j)], send_r.at[j], recv_l.at[j], right)

    def to_left(j):
        piece = (j + half) % own_pieces
        return remote(own_piece(piece), xg_ref.at[rows_at(me, piece)], send_l.at[j], recv_r.at[j], left)

    own_to_partner = remote(
        x_ref, xg_ref.at[pl.ds(pl.multiple_of(me * chunk, chunk), chunk)],
        send_p.at[2 * arrivals], recv_p.at[2 * arrivals], partner,
    )

    def start_own(j):
        to_right(j).start()
        to_left(j).start()

    own_to_partner.start()
    each(own_pieces, start_own)

    def from_left(j, c):
        return rows_at((chip + chips - 1 - j // own_pieces) % chips * CORES + c, j % own_pieces)

    def from_right(j, c):
        return rows_at((chip + 1 + j // own_pieces) % chips * CORES + c, (j + half) % own_pieces)

    def group_rows(g, i):
        j = g - first
        in_chunk = (g % own_groups) * per_group + i
        dev = jnp.where(g < own_groups, me, partner)
        early = dev * chunk + in_chunk * PIECE
        c = core if i < 2 else 1 - core
        if i % 2 == 0:
            late = ((chip + chips - 1 - j // own_pieces) % chips * CORES + c) * chunk + j % own_pieces * PIECE
        else:
            late = ((chip + 1 + j // own_pieces) % chips * CORES + c) * chunk + (j + half) % own_pieces * PIECE
        return early, late

    def lhs_copy(src, slot, i):
        return pltpu.make_async_copy(src, lhs.at[slot, pl.ds(i * PIECE, PIECE)], lhs_sem.at[slot, i])

    def relay_left(j):
        return remote(
            xg_ref.at[from_left(j, core)], xg_ref.at[from_left(j, core)],
            send_r.at[own_pieces + j], recv_l.at[own_pieces + j], right,
        )

    def relay_right(j):
        return remote(
            xg_ref.at[from_right(j, core)], xg_ref.at[from_right(j, core)],
            send_l.at[own_pieces + j], recv_r.at[own_pieces + j], left,
        )

    def share(j, side):
        rows = from_left(j, core) if side == 0 else from_right(j, core)
        return remote(xg_ref.at[rows], xg_ref.at[rows], send_p.at[2 * j + side], recv_p.at[2 * j + side], partner)

    def shared(j, side):
        rows = from_left(j, 1 - core) if side == 0 else from_right(j, 1 - core)
        return remote(xg_ref.at[rows], xg_ref.at[rows], send_p.at[2 * j + side], recv_p.at[2 * j + side], partner)

    def landed(rows, sem):
        return remote(xg_ref.at[rows], xg_ref.at[rows], sem, sem, partner)

    def fetch_links(g):
        slot = g % 2

        @pl.when(g < own_groups)
        def _():
            for i in range(per_group):
                lhs_copy(own_piece(g * per_group + i), slot, i).start()

        @pl.when((g >= own_groups) & (g < first))
        def _():
            @pl.when(g == own_groups)
            def _():
                own_to_partner.wait_recv()

            for i in range(per_group):
                lhs_copy(xg_ref.at[rows_at(partner, (g - own_groups) * per_group + i)], slot, i).start()

        @pl.when(g >= first)
        def _():
            j = g - first
            landed(from_left(j, core), recv_l.at[j]).wait_recv()
            landed(from_right(j, core), recv_r.at[j]).wait_recv()

            @pl.when(j < half)
            def _():
                relay_left(j).start()
                relay_right(j).start()

            share(j, 0).start()
            share(j, 1).start()
            lhs_copy(xg_ref.at[from_left(j, core)], slot, 0).start()
            lhs_copy(xg_ref.at[from_right(j, core)], slot, 1).start()

    def fetch_partner(g):
        @pl.when(g >= first)
        def _():
            j = g - first
            slot = g % 2
            shared(j, 0).wait_recv()
            shared(j, 1).wait_recv()
            lhs_copy(xg_ref.at[from_left(j, 1 - core)], slot, 2).start()
            lhs_copy(xg_ref.at[from_right(j, 1 - core)], slot, 3).start()

    def out_copies(g, i):
        slot = g % 2
        early, late = group_rows(g, i)
        rows = pl.ds(pl.multiple_of(jnp.where(g < first, early, late), PIECE), PIECE)
        part = pl.ds(i * PIECE, PIECE)
        return (
            pltpu.make_async_copy(qo.at[slot, part], qkv_ref.at[rows], qo_sem.at[slot, i]),
            pltpu.make_async_copy(ho.at[slot, part], h_ref.at[rows], ho_sem.at[slot, i]),
        )

    def wait_out(g):
        for i in range(per_group):
            for copy in out_copies(g, i):
                copy.wait()

    qkv_width = wq_v.shape[1]
    ff_width = w1_v.shape[0]

    def compute(g):
        slot = g % 2
        for i in range(per_group):
            lhs_copy(own_piece(i), slot, i).wait()

        @pl.when(g >= 2)
        def _():
            wait_out(g - 2)

        @pl.when(g == 0)
        def _():
            load_q.wait()

        def qkv_tile(n):
            cols = pl.ds(pl.multiple_of(n * COLS, COLS), COLS)
            qo[slot, :, cols] = jnp.dot(lhs[slot], wq_v[:, cols], preferred_element_type=jnp.float32).astype(qo.dtype)

        each(qkv_width // COLS, qkv_tile)

        @pl.when(g == 0)
        def _():
            load_1.wait()

        def up(rows):
            pre = lax.dot_general(lhs[slot], w1_v[rows, :], (((1,), (1,)), ((), ())), preferred_element_type=jnp.float32)
            return jax.nn.gelu(pre, approximate=True).astype(ho.dtype)

        def up_tile(n):
            cols = pl.ds(pl.multiple_of(n * COLS, COLS), COLS)
            ho[slot, :, cols] = up(cols)

        each(ff_width // COLS, up_tile)
        done = ff_width // COLS * COLS
        if done < ff_width:
            ho[slot, :, done:] = up(pl.ds(done, ff_width - done))
        for i in range(per_group):
            for copy in out_copies(g, i):
                copy.start()

    load_q.start()
    load_1.start()
    fetch_links(jnp.int32(0))

    def step(g):
        @pl.when(g < groups - 3)
        def _():
            fetch_links(g + 1)

        compute(g)

        @pl.when((g >= groups - 3) & (g < groups - 1))
        def _():
            fetch_links(g + 1)

        @pl.when(g < groups - 1)
        def _():
            fetch_partner(g + 1)

    each(groups, step)

    wait_out(jnp.int32(groups - 2))
    wait_out(jnp.int32(groups - 1))
    own_to_partner.wait_send()

    def finish_own(j):
        to_right(j).wait_send()
        to_left(j).wait_send()

    def finish_relay(j):
        relay_left(j).wait_send()
        relay_right(j).wait_send()

    def finish_share(j):
        share(j, 0).wait_send()
        share(j, 1).wait_send()

    each(own_pieces, finish_own)
    each(half, finish_relay)
    each(arrivals, finish_share)


def gather_project(chips, normed, w_qkv, w_up_t):
    chunk, width = normed.shape
    tokens = chunk * chips * CORES
    qkv_width, ff_width = w_qkv.shape[1], w_up_t.shape[0]
    arrivals = chunk // PIECE + chunk // PIECE // 2
    dma = pltpu.SemaphoreType.DMA
    out = pl.pallas_call(
        functools.partial(gather_kernel, chips),
        in_specs=[ANY] * 3,
        out_specs=[ANY] * 3,
        out_shape=[
            jax.ShapeDtypeStruct((tokens, width), jnp.bfloat16),
            jax.ShapeDtypeStruct((tokens, qkv_width), jnp.bfloat16),
            jax.ShapeDtypeStruct((tokens, ff_width), jnp.bfloat16),
        ],
        scratch_shapes=[
            pltpu.VMEM(w_qkv.shape, jnp.bfloat16),
            pltpu.VMEM(w_up_t.shape, jnp.bfloat16),
            pltpu.VMEM((2, BLOCK, width), jnp.bfloat16),
            pltpu.VMEM((2, BLOCK, qkv_width), jnp.bfloat16),
            pltpu.VMEM((2, BLOCK, ff_width), jnp.bfloat16),
            dma((2,)), dma((2, BLOCK // PIECE)), dma((2, BLOCK // PIECE)), dma((2, BLOCK // PIECE)),
            dma((arrivals,)), dma((arrivals,)), dma((arrivals,)), dma((arrivals,)),
            dma((2 * arrivals + 1,)), dma((2 * arrivals + 1,)),
        ],
        compiler_params=pltpu.CompilerParams(collective_id=0, has_side_effects=True, vmem_limit_bytes=VMEM_LIMIT),
        name="gather_project",
    )(normed, w_qkv, w_up_t)
    return out[1], out[2]


def attend_kernel(
    chips, heads, head_dim, qkv_ref, h_ref, x_ref, wo_ref, w2_ref,
    y_ref, rp_ref, ro_ref, rn_ref, ps_ref,
    qkv_v, wo_v, w2_v, s_v, o_v, h_v, acc, stage, x_v, y_v,
    w_sem, h_sem, st_sem, x_sem, y_sem, ps_sem, send_p, recv_p, send_o, recv_o, send_n, recv_n,
):
    me, chip, core, right, left, partner = neighbours(chips)
    chunk, width = x_ref.shape
    tokens = qkv_v.shape[0]
    blocks = chunk // BLOCK
    pairs = chips * blocks
    half = width // 2
    slices = BLOCK // PIECE
    key_tile = min(tokens, 1024)
    factor = head_dim ** -0.5 * math.log2(math.e)

    greet((right, left, partner))

    load_qkv = pltpu.make_async_copy(qkv_ref, qkv_v, w_sem.at[0])
    load_wo = pltpu.make_async_copy(wo_ref, wo_v, w_sem.at[1])
    load_w2 = pltpu.make_async_copy(w2_ref, w2_v, w_sem.at[2])
    load_qkv.start()
    load_wo.start()
    load_w2.start()

    def place(p):
        quarter = p // blocks
        mid = (quarter + 1) // 2 % 2
        offset = mid * (1 + 2 * (p % 2)) + (1 - mid) * (2 - 2 * (quarter // 3))
        block = mid * (quarter - 1) + (1 - mid) * (p % 2)
        return offset, block

    def block_rows(i, size=BLOCK):
        return pl.ds(pl.multiple_of(i * size, size), size)

    def token_block(s):
        p = s // 2
        offset, block = place(p)
        device = (chip + offset) % chips * CORES + (core + 1 - s % 2) % 2
        return device * blocks + block

    def to_partner(p):
        return remote(acc.at[0], rp_ref.at[block_rows(p)], send_p.at[p], recv_p.at[p], partner)

    def to_side(p, side):
        src = ps_ref.at[block_rows(p), pl.ds(side * half, half)]
        dst = ro_ref.at[block_rows(side * blocks + p)]
        return remote(src, dst, send_o.at[side, p], recv_o.at[side, p], left if side else right)

    def to_owner(p, k):
        side = p % 2
        offset, block = place(p)
        src = ps_ref.at[block_rows(p * slices + k, PIECE)]
        dst = rn_ref.at[block_rows((side * blocks + block) * slices + k, PIECE)]
        device = (chip + offset) % chips * CORES + core
        return remote(src, dst, send_n.at[side, block * slices + k], recv_n.at[side, block * slices + k], device)

    def owner_part(side, block, k):
        rows = block_rows((side * blocks + block) * slices + k, PIECE)
        return rn_ref.at[rows], recv_n.at[side, block * slices + k]

    def attend_head(row, head):
        base = pl.multiple_of(head * 3 * head_dim, head_dim)
        q = qkv_v[row, pl.ds(base, head_dim)]
        k_cols = pl.ds(pl.multiple_of(base + head_dim, head_dim), head_dim)
        v_cols = pl.ds(pl.multiple_of(base + 2 * head_dim, head_dim), head_dim)
        top = None
        for t in range(tokens // key_tile):
            keys = pl.ds(t * key_tile, key_tile)
            s = lax.dot_general(q, qkv_v[keys, k_cols], (((1,), (1,)), ((), ())), preferred_element_type=jnp.float32)
            s_v[:, keys] = s
            tile_top = jnp.max(s, axis=-1, keepdims=True)
            top = tile_top if top is None else jnp.maximum(top, tile_top)
        total, out = None, None
        for t in range(tokens // key_tile):
            keys = pl.ds(t * key_tile, key_tile)
            e = jnp.exp2((s_v[:, keys] - top) * factor)
            tile_sum = jnp.sum(e, axis=-1, keepdims=True)
            tile_out = jnp.dot(e.astype(jnp.bfloat16), qkv_v[keys, v_cols], preferred_element_type=jnp.float32)
            total = tile_sum if total is None else total + tile_sum
            out = tile_out if out is None else out + tile_out
        o_v[:, pl.ds(pl.multiple_of(head * head_dim, head_dim), head_dim)] = (out / total).astype(o_v.dtype)

    def load_h(s):
        return pltpu.make_async_copy(h_ref.at[block_rows(token_block(s))], h_v, h_sem)

    def stage_partner(p):
        return pltpu.make_async_copy(rp_ref.at[block_rows(p)], stage.at[0], st_sem.at[0])

    def stage_side(side, block):
        return pltpu.make_async_copy(
            ro_ref.at[block_rows(side * blocks + block)], stage.at[1, :, pl.ds(0, half)], st_sem.at[1]
        )

    def spill(p):
        return pltpu.make_async_copy(acc.at[1], ps_ref.at[block_rows(p)], ps_sem)

    def step(s):
        p = s // 2
        mine = s % 2
        offset, block = place(p)
        is_mid = (offset % 2) == 1
        load_h(s).start()

        @pl.when(s == 0)
        def _():
            load_qkv.wait()

        row = block_rows(token_block(s))
        each(heads, lambda head: attend_head(row, head))
        load_h(s).wait()

        @pl.when(s == 0)
        def _():
            load_wo.wait()
            load_w2.wait()

        @pl.when((mine == 0) & (p > 0))
        def _():
            to_partner(p - 1).wait_send()

        @pl.when(mine == 1)
        def _():
            to_partner(p).wait_recv()
            stage_partner(p).start()

            @pl.when(is_mid)
            def _():
                side = p % 2
                pltpu.make_async_remote_copy(
                    src_ref=ro_ref.at[block_rows(side * blocks + block)], dst_ref=ro_ref.at[block_rows(side * blocks + block)],
                    send_sem=send_o.at[side, block], recv_sem=recv_o.at[side, block],
                    device_id={"tp": partner}, device_id_type=MESH,
                ).wait_recv()
                stage_side(side, block).start()

        def project(n):
            cols = pl.ds(pl.multiple_of(n * COLS, COLS), COLS)
            acc[mine, :, cols] = jnp.dot(
                o_v[...], wo_v[:, cols], preferred_element_type=jnp.float32
            ) + jnp.dot(h_v[...], w2_v[:, cols], preferred_element_type=jnp.float32)

        each(width // COLS, project)

        @pl.when(mine == 0)
        def _():
            to_partner(p).start()

        @pl.when(mine == 1)
        def _():
            stage_partner(p).wait()

            def add(n):
                cols = pl.ds(pl.multiple_of(n * COLS, COLS), COLS)
                acc[1, :, cols] += stage[0, :, cols]

            each(width // COLS, add)

            @pl.when(is_mid)
            def _():
                side = p % 2
                stage_side(side, block).wait()

                def add_side(n):
                    dst = pl.ds(pl.multiple_of(side * half + n * COLS, COLS), COLS)
                    src = pl.ds(pl.multiple_of(n * COLS, COLS), COLS)
                    acc[1, :, dst] += stage[1, :, src]

                each(half // COLS, add_side)

            @pl.when(offset != 0)
            def _():
                spill(p).start()
                spill(p).wait()

                @pl.when(is_mid)
                def _():
                    each(slices, lambda k: to_owner(p, k).start())

                @pl.when(offset == 2)
                def _():
                    to_side(p, 0).start()
                    to_side(p, 1).start()

            @pl.when(offset == 0)
            def _():
                def final(k):
                    rows = block_rows(block * slices + k, PIECE)
                    load_x = pltpu.make_async_copy(x_ref.at[rows], x_v, x_sem)
                    load_x.start()
                    copies = []
                    for side in range(2):
                        src, sem = owner_part(side, block, k)
                        remote(src, src, sem, sem, partner).wait_recv()
                        copy = pltpu.make_async_copy(src, stage.at[side, pl.ds(0, PIECE)], st_sem.at[side])
                        copy.start()
                        copies.append(copy)
                    load_x.wait()
                    for copy in copies:
                        copy.wait()

                    def finish(n):
                        cols = pl.ds(pl.multiple_of(n * COLS, COLS), COLS)
                        summed = acc[1, block_rows(k, PIECE), cols] + stage[0, pl.ds(0, PIECE), cols] + stage[1, pl.ds(0, PIECE), cols]
                        y_v[:, cols] = (x_v[:, cols].astype(jnp.float32) + summed).astype(y_v.dtype)

                    each(width // COLS, finish)
                    store = pltpu.make_async_copy(y_v, y_ref.at[rows], y_sem)
                    store.start()
                    store.wait()

                each(slices, final)

    each(2 * pairs, step)
    to_partner(pairs - 1).wait_send()
    for p in range(blocks):
        to_side(p, 0).wait_send()
        to_side(p, 1).wait_send()
    for p in range(blocks, 3 * blocks):
        each(slices, lambda k, p=p: to_owner(p, k).wait_send())


def attend_reduce(chips, heads, head_dim, qkv, hidden, x_loc, w_out, w_down):
    chunk, width = x_loc.shape
    tokens, qkv_width = qkv.shape
    ff_width = hidden.shape[1]
    blocks = chunk // BLOCK
    slices = BLOCK // PIECE
    pairs = chips * blocks
    f32 = jnp.float32
    dma = pltpu.SemaphoreType.DMA
    out = pl.pallas_call(
        functools.partial(attend_kernel, chips, heads, head_dim),
        in_specs=[ANY] * 5,
        out_specs=[ANY] * 5,
        out_shape=[
            jax.ShapeDtypeStruct((chunk, width), jnp.bfloat16),
            jax.ShapeDtypeStruct((pairs * BLOCK, width), f32),
            jax.ShapeDtypeStruct((2 * chunk, width // 2), f32),
            jax.ShapeDtypeStruct((2 * chunk, width), f32),
            jax.ShapeDtypeStruct((3 * chunk, width), f32),
        ],
        scratch_shapes=[
            pltpu.VMEM((tokens, qkv_width), jnp.bfloat16),
            pltpu.VMEM(w_out.shape, jnp.bfloat16),
            pltpu.VMEM(w_down.shape, jnp.bfloat16),
            pltpu.VMEM((BLOCK, tokens), f32),
            pltpu.VMEM((BLOCK, w_out.shape[0]), jnp.bfloat16),
            pltpu.VMEM((BLOCK, ff_width), jnp.bfloat16),
            pltpu.VMEM((2, BLOCK, width), f32),
            pltpu.VMEM((2, BLOCK, width), f32),
            pltpu.VMEM((PIECE, width), jnp.bfloat16),
            pltpu.VMEM((PIECE, width), jnp.bfloat16),
            dma((3,)), dma, dma((2,)), dma, dma, dma,
            dma((pairs,)), dma((pairs,)),
            dma((2, blocks)), dma((2, blocks)),
            dma((2, blocks * slices)), dma((2, blocks * slices)),
        ],
        compiler_params=pltpu.CompilerParams(collective_id=1, has_side_effects=True, vmem_limit_bytes=VMEM_LIMIT),
        name="attend_reduce",
    )(qkv, hidden, x_loc, w_out, w_down)
    return out[0]


def solution(mesh):
    chips = mesh.shape["tp"] // CORES

    def local_block(x_loc, ln_gamma, w_qkv, w_out, w_up, w_down):
        model_dim = x_loc.shape[1]
        heads, head_dim = w_out.shape[0], w_out.shape[1]
        normed = layer_norm(x_loc, ln_gamma)
        qkv, hidden = gather_project(chips, normed, w_qkv.reshape(model_dim, heads * 3 * head_dim), w_up.T)
        return attend_reduce(chips, heads, head_dim, qkv, hidden, x_loc, w_out.reshape(heads * head_dim, model_dim), w_down)

    row_spec = P(("data", "tp"), None)
    return jax.shard_map(local_block, mesh=mesh, in_specs=(row_spec, P(None), P(None, "tp", None), P("tp", None, None), P(None, "tp"), P("tp", None)), out_specs=row_spec, check_vma=False)
```

time: 1030 us -> 498 us (0.48)
  waiting for transfers between devices: 481 us -> 0 us
  Pallas kernels: 0 us -> 480 us
  matrix products: 419 us -> 0 us
  other arithmetic: 104 us -> 0 us
  between operations: 13.9 us -> 0.02 us
  local copies, waits for them, and re-layouts: 4.93 us -> 17.2 us
    pallas_call x0 -> x3, Pallas kernels: none -> 480 us  [the longest x1 312 us: attend_reduce(): pl.pallas_call(functools.partial(attend_kernel, chips, heads, head_dim),...]
    dot_general x12 -> x0, matrix products: 419 us -> none  [the longest x4 105 us: one_block(): jnp.einsum('qhe,khe->hqk', query_blk, key_rows, preferred_element_type=jn...]
    reduce_scatter x1 -> x0, waiting for transfers between devices: 325 us -> none  [local_block(): reduced = lax.psum_scatter(part_sum, 'tp', scatter_dimension=0, tiled=True)]
    all_gather x1 -> x0, waiting for transfers between devices: 156 us -> none  [local_block(): gathered = lax.all_gather(normed, 'tp', axis=0, tiled=True)]
    reduce_sum x6 -> x0, other arithmetic: 91.3 us -> none  [the longest x4 84.9 us: one_block(): exp_sum = jnp.sum(exp_scores, axis=-1, keepdims=True)]
    unnamed x2, local copies, waits for them, and re-layouts: 0.01 us -> 17.2 us
    convert_element_type x2 -> x0, other arithmetic: 13 us -> none  [the longest x1 8 us: local_block(): return (residual + reduced).astype(jnp.bfloat16)]
  transfers between devices with their start and end apart: 2 -> 0, of which waited for: 2 -> 0; matrix products, arithmetic and copies ran while one was open for 0% -> 0% of each run, Pallas kernels for 0% -> 0%
where the time goes in v1:
time: 498 us; the launch traced here: 497 us
  Pallas kernels  480 us (96%)
  local copies, waits for them, and re-layouts  17.2 us (3%)
    pallas_call x1, Pallas kernels, attend_reduce(): pl.pallas_call(functools.partial(attend_kernel, chips, heads, head_dim),...  312 us
    pallas_call x1, Pallas kernels, gather_project(): pl.pallas_call(functools.partial(gather_kernel, chips), in_specs=[ANY] *...  161 us
    unnamed x2, local copies, waits for them, and re-layouts  17.2 us

profile of v1, /device:TPU:112, one launch (start us, length us, event | category | flops | bytes accessed | tf_op | source)
XLA Modules:
  0.0 496.8 jit_solution(1657244268820816335)
XLA Ops:
  0.0 6.6 %norm.1.x_ref = bf16[512,4096]{1,0:T(8,128)(2,1)} custom-call(bf16[512,4096]{1,0:T(8,128)(2,1)} %x_ref.3, f32[1,4096]{1,0:T(1,128)} %bitcast.9), custom_call_target="tpu_custom_call" | custom-call | tf_op jit(solution)/shard_map/norm/pallas_call | solution.py:31
  6.6 12.5 %copy.7 = bf16[512,8,4,384]{3,1,2,0:T(8,128)(2,1)} copy(bf16[512,8,4,384]{3,2,1,0:T(4,128)(2,1)} %bitcast.6) | data formatting | bytes 25165824
  19.1 160.8 %gather_project.1 = (bf16[4096,4096]{1,0:T(8,128)(2,1)}, bf16[4096,1536]{1,0:T(8,128)(2,1)}, bf16[4096,1376]{1,0:T(8,128)(2,1)}) custom-call(bf16[512,4096]{1,0:T(8,128)(2,1)} %norm.1.x_ref, bf16[4096,1536]{1,0:T(8,128)(2,1)} %bitcast.5, bf16[1376,4096]{1,0:T(8,128)(2,1)} %bitcast.7), custom_call_target="tpu_custom_call" | custom-call | tf_op jit(solution)/shard_map/gather_project/pallas_call | solution.py:307
  179.9 312.2 %attend_reduce.1 = (bf16[512,4096]{1,0:T(8,128)(2,1)}, f32[2048,4096]{1,0:T(8,128)}, f32[1024,2048]{1,0:T(8,128)}, f32[1024,4096]{1,0:T(8,128)}, f32[1536,4096]{1,0:T(8,128)}) custom-call(bf16[4096,1536]{1,0:T(8,128)(2,1)} %get-tuple-element.8.qkv_ref, bf16[4096,1376]{1,0:T(8,128)(2,1)} %get-tuple-element.9.h_ref, bf16[512,4096]{1,0:T(8,128)(2,1)} %x_ref.3, ...), custom_call_target="tpu_custom_call" | custom-call | tf_op jit(solution)/shard_map/attend_reduce/pallas_call | solution.py:563
  492.1 4.7 copy.9

commit v2 on v0

v2 whole, which is shorter than its diff:
```python
import functools
import math

import jax
import jax.numpy as jnp
from jax import lax
from jax.experimental import pallas as pl
from jax.experimental.pallas import tpu as pltpu
from jax.sharding import PartitionSpec as P

LN_EPS = 1e-6
MESH = pl.DeviceIdType.MESH
CORES = 2
PIECE = 64
GROUP = 256
BLOCK = 256
FIRST = 128
REPACK = 256
LATE = 3
COLS = 2048
LANES = 512
VMEM_LIMIT = 67_000_000
ANY = pl.BlockSpec(memory_space=pl.ANY)


def neighbours(chips):
    me = lax.axis_index("tp")
    chip, core = me // CORES, me % CORES
    right = (chip + 1) % chips * CORES + core
    left = (chip + chips - 1) % chips * CORES + core
    partner = chip * CORES + (1 - core)
    return me, chip, core, right, left, partner


def greet(devices):
    barrier = pltpu.get_barrier_semaphore()
    for device in devices:
        pl.semaphore_signal(barrier, inc=1, device_id={"tp": device}, device_id_type=MESH)
    pl.semaphore_wait(barrier, len(devices))


def remote(src, dst, send_sem, recv_sem, device):
    return pltpu.make_async_remote_copy(
        src_ref=src, dst_ref=dst, send_sem=send_sem, recv_sem=recv_sem, device_id={"tp": device}, device_id_type=MESH
    )


def each(count, body):
    def step(i, carry):
        body(i)
        return carry

    lax.fori_loop(0, count, step, 0)


def block_kernel(
    chips, x_ref, gamma_ref, wq_ref, wo_ref, w1_ref, w2_ref,
    y_ref, xg_ref, h_ref, rp_ref, ro_ref, rn_ref, ps_ref,
    qkv_v, wo_v, w2_v, gamma_v,
    w_sem, x_sem, wq_sem, lhs_sem, ho_sem, send_r, recv_l, send_l, recv_r, send_g, recv_g,
    h_sem, st_sem, xr_sem, y_sem, ps_sem, send_p, recv_p, send_o, recv_o, send_n, recv_n,
):
    me, chip, core, right, left, partner = neighbours(chips)
    chunk, width = x_ref.shape
    heads, qkv_head = wq_ref.shape[1], wq_ref.shape[2]
    load_wo = pltpu.make_async_copy(wo_ref, wo_v, w_sem.at[1])
    load_w2 = pltpu.make_async_copy(w2_ref, w2_v, w_sem.at[2])
    bf16, f32 = jnp.bfloat16, jnp.float32

    def project_phase(wq_v, w1_v, w4_v, lhs, ho):
        own_pieces = chunk // PIECE
        half = own_pieces // 2
        arrivals = own_pieces + half
        per_group = GROUP // PIECE
        own_groups = chunk // GROUP
        first = own_groups * CORES
        groups = first + arrivals

        load_x = [pltpu.make_async_copy(x_ref.at[pl.ds(i * GROUP, GROUP)], lhs.at[i], x_sem.at[i]) for i in range(own_groups)]
        for copy in load_x:
            copy.start()
        load_gamma = pltpu.make_async_copy(gamma_ref, gamma_v, w_sem.at[3])
        load_gamma.start()

        def load_wq(i):
            rows = pl.ds(pl.multiple_of(i * REPACK, REPACK), REPACK)
            return pltpu.make_async_copy(wq_ref.at[rows], w4_v.at[i % 2], wq_sem.at[i % 2])

        load_w1 = pltpu.make_async_copy(w1_ref, w1_v, w_sem.at[0])
        load_wq(0).start()
        load_w1.start()
        greet((right, left, partner))

        def rows_at(device, piece):
            return pl.ds(pl.multiple_of(device * chunk + piece * PIECE, PIECE), PIECE)

        def own_send(piece, sends, recvs, j, device):
            rows = xg_ref.at[rows_at(me, piece)]
            return remote(rows, rows, sends.at[j], recvs.at[j], device)

        def to_right(j):
            return own_send(j, send_r, recv_l, j, right)

        def to_left(j):
            return own_send((j + half) % own_pieces, send_l, recv_r, j, left)

        def own_to_partner():
            rows = xg_ref.at[pl.ds(pl.multiple_of(me * chunk, chunk), chunk)]
            return remote(rows, rows, send_g.at[2 * arrivals], recv_g.at[2 * arrivals], partner)

        def normalise(j):
            out = []
            for side in range(2):
                rows = pl.ds(pl.multiple_of(j * PIECE, PIECE), PIECE)
                vals = lhs[side, rows, :].astype(f32)
                centered = vals - jnp.mean(vals, axis=-1, keepdims=True)
                var = jnp.mean(centered * centered, axis=-1, keepdims=True)
                lhs[side, rows, :] = (centered * lax.rsqrt(var + LN_EPS) * gamma_v[...]).astype(bf16)
                piece = j + side * half
                copy = pltpu.make_async_copy(lhs.at[side, rows], xg_ref.at[rows_at(me, piece)], lhs_sem.at[side, 0])
                copy.start()
                out.append(copy)
            for copy in out:
                copy.wait()

        for copy in load_x:
            copy.wait()
        load_gamma.wait()

        def open_links(j):
            normalise(j)
            to_right(j).start()
            to_left(j).start()

        each(half, open_links)
        own_to_partner().start()

        def open_rest(j):
            to_right(half + j).start()
            to_left(half + j).start()

        each(half, open_rest)
        load_wo.start()
        load_w2.start()

        def repack(i):
            @pl.when(i < width // REPACK - 1)
            def _():
                load_wq(i + 1).start()

            load_wq(i).wait()
            rows = pl.ds(pl.multiple_of(i * REPACK, REPACK), REPACK)
            wq_v[rows, :] = w4_v[i % 2].reshape(REPACK, heads * qkv_head)

        each(width // REPACK, repack)
        load_w1.wait()

        def left_row(j, c):
            return ((chip + chips - 1 - j // own_pieces) % chips * CORES + c) * chunk + j % own_pieces * PIECE

        def right_row(j, c):
            return ((chip + 1 + j // own_pieces) % chips * CORES + c) * chunk + (j + half) % own_pieces * PIECE

        def side_rows(j, side, c):
            row = right_row(j, c) if side else left_row(j, c)
            return pl.ds(pl.multiple_of(row, PIECE), PIECE)

        def lhs_copy(src, slot, i):
            return pltpu.make_async_copy(src, lhs.at[slot, pl.ds(i * PIECE, PIECE)], lhs_sem.at[slot, i])

        def relay(j, side):
            rows = xg_ref.at[side_rows(j, side, core)]
            sends, recvs, device = (send_l, recv_r, left) if side else (send_r, recv_l, right)
            return remote(rows, rows, sends.at[own_pieces + j], recvs.at[own_pieces + j], device)

        def share(j, side, c):
            rows = xg_ref.at[side_rows(j, side, c)]
            return remote(rows, rows, send_g.at[2 * j + side], recv_g.at[2 * j + side], partner)

        def fetch_links(g):
            slot = g % 2

            @pl.when((g >= own_groups) & (g < first))
            def _():
                @pl.when(g == own_groups)
                def _():
                    own_to_partner().wait_recv()

                for i in range(per_group):
                    lhs_copy(xg_ref.at[rows_at(partner, (g - own_groups) * per_group + i)], slot, i).start()

            @pl.when(g >= first)
            def _():
                j = g - first
                for side in range(2):
                    rows = xg_ref.at[side_rows(j, side, core)]
                    sem = (recv_r if side else recv_l).at[j]
                    remote(rows, rows, sem, sem, partner).wait_recv()

                @pl.when(j < half)
                def _():
                    relay(j, 0).start()
                    relay(j, 1).start()

                for side in range(2):
                    share(j, side, core).start()
                    lhs_copy(xg_ref.at[side_rows(j, side, core)], slot, side).start()

        def fetch_partner(g):
            @pl.when(g >= first)
            def _():
                j = g - first
                for side in range(2):
                    share(j, side, 1 - core).wait_recv()
                for side in range(2):
                    lhs_copy(xg_ref.at[side_rows(j, side, 1 - core)], g % 2, 2 + side).start()

        def group_row(g, i):
            j = g - first
            early = jnp.where(g < own_groups, me, partner) * chunk + ((g % own_groups) * per_group + i) * PIECE
            c = core if i < 2 else 1 - core
            late = right_row(j, c) if i % 2 else left_row(j, c)
            return pl.ds(pl.multiple_of(jnp.where(g < first, early, late), PIECE), PIECE)

        def out_copy(g, i):
            slot = g % 2
            return pltpu.make_async_copy(ho.at[slot, pl.ds(i * PIECE, PIECE)], h_ref.at[group_row(g, i)], ho_sem.at[slot, i])

        def wait_out(g):
            for i in range(per_group):
                out_copy(g, i).wait()

        def compute_qkv(g):
            slot = g % 2

            @pl.when(g >= own_groups)
            def _():
                for i in range(per_group):
                    lhs_copy(xg_ref.at[rows_at(me, i)], slot, i).wait()

            @pl.when(g >= 2)
            def _():
                wait_out(g - 2)

            tile = jnp.dot(lhs[slot], wq_v[...], preferred_element_type=f32).astype(bf16)
            for i in range(per_group):
                qkv_v[group_row(g, i), :] = tile[i * PIECE:(i + 1) * PIECE]

        def compute_up(g):
            slot = g % 2
            pre = lax.dot_general(lhs[slot], w1_v[...], (((1,), (1,)), ((), ())), preferred_element_type=f32)
            ho[slot] = jax.nn.gelu(pre, approximate=True).astype(bf16)
            for i in range(per_group):
                out_copy(g, i).start()

        def step(g):
            ahead = g < groups - LATE

            @pl.when(ahead)
            def _():
                fetch_links(g + 1)

            compute_qkv(g)

            @pl.when(ahead)
            def _():
                fetch_partner(g + 1)

            compute_up(g)

            @pl.when(jnp.logical_not(ahead) & (g < groups - 1))
            def _():
                fetch_links(g + 1)
                fetch_partner(g + 1)

        each(groups, step)
        wait_out(jnp.int32(groups - 2))
        wait_out(jnp.int32(groups - 1))

        own_to_partner().wait_send()

        def finish_own(j):
            to_right(j).wait_send()
            to_left(j).wait_send()

        def finish_relay(j):
            relay(j, 0).wait_send()
            relay(j, 1).wait_send()

        def finish_share(j):
            share(j, 0, core).wait_send()
            share(j, 1, core).wait_send()

        each(own_pieces, finish_own)
        each(half, finish_relay)
        each(arrivals, finish_share)

    def attend_phase(s_v, o_v, h_v, acc, stage, x_v, y_v):
        head_dim = qkv_head // 3
        tokens = qkv_v.shape[0]
        firsts = chunk // FIRST
        blocks = chunk // BLOCK
        half = width // 2
        slices = BLOCK // PIECE
        factor = head_dim ** -0.5 * math.log2(math.e)

        def block_rows(i, size):
            return pl.ds(pl.multiple_of(i * size, size), size)

        def to_partner(p, i, size, side):
            cols = pl.ds(side * half, half)
            src = acc.at[0, pl.ds(0, size), cols]
            dst = rp_ref.at[block_rows(i, size), cols]
            return remote(src, dst, send_p.at[p, side], recv_p.at[p, side], partner)

        def to_side(b, side):
            src = ps_ref.at[block_rows(b, FIRST), pl.ds(side * half, half)]
            dst = ro_ref.at[block_rows(side * firsts + b, FIRST)]
            return remote(src, dst, send_o.at[side, b], recv_o.at[side, b], left if side else right)

        def to_owner(q, k):
            side, block = q % 2, q // 2
            i = block * slices + k
            src = ps_ref.at[block_rows(firsts * FIRST // PIECE + q * slices + k, PIECE)]
            dst = rn_ref.at[block_rows(side * blocks * slices + i, PIECE)]
            device = (chip + 1 + 2 * side) % chips * CORES + core
            return remote(src, dst, send_n.at[side, i], recv_n.at[side, i], device)

        def attend_head(size, row, head):
            base = pl.multiple_of(head * qkv_head, head_dim)
            q = qkv_v[row, pl.ds(base, head_dim)]
            k_cols = pl.ds(pl.multiple_of(base + head_dim, head_dim), head_dim)
            v_cols = pl.ds(pl.multiple_of(base + 2 * head_dim, head_dim), head_dim)
            s = lax.dot_general(q, qkv_v[:, k_cols], (((1,), (1,)), ((), ())), preferred_element_type=f32)
            s_v[pl.ds(0, size), :] = s
            top = jnp.max(s, axis=-1, keepdims=True)
            e = jnp.exp2((s_v[pl.ds(0, size), :] - top) * factor)
            total = jnp.sum(e, axis=-1, keepdims=True)
            out = jnp.dot(e.astype(bf16), qkv_v[:, v_cols], preferred_element_type=f32)
            o_v[pl.ds(0, size), pl.ds(pl.multiple_of(head * head_dim, head_dim), head_dim)] = (out / total).astype(bf16)

        def partial(size, device, block, mine, between, after):
            row = block_rows(device * (chunk // size) + block, size)
            part = pl.ds(0, size)
            load_h = pltpu.make_async_copy(h_ref.at[row], h_v.at[part], h_sem)
            load_h.start()
            each(heads, lambda head: attend_head(size, row, head))
            load_h.wait()
            between()
            for n in range(width // COLS):
                cols = pl.ds(n * COLS, COLS)
                acc[mine, part, cols] = jnp.dot(
                    o_v[part, :], wo_v[:, cols], preferred_element_type=f32
                ) + jnp.dot(h_v[part, :], w2_v[:, cols], preferred_element_type=f32)
                after(n)

        def stage_partner(i, size):
            return pltpu.make_async_copy(rp_ref.at[block_rows(i, size)], stage.at[0, pl.ds(0, size)], st_sem.at[0])

        def stage_side(side, block):
            src = ro_ref.at[block_rows(side * blocks + block, BLOCK)]
            return pltpu.make_async_copy(src, stage.at[1, :, pl.ds(0, half)], st_sem.at[1])

        def add(size, base, slot, count):
            def tile(n):
                dst = pl.ds(pl.multiple_of(base + n * LANES, LANES), LANES)
                src = pl.ds(pl.multiple_of(n * LANES, LANES), LANES)
                acc[1, pl.ds(0, size), dst] += stage[slot, pl.ds(0, size), src]

            each(count // LANES, tile)

        def spill(i, size):
            return pltpu.make_async_copy(acc.at[1, pl.ds(0, size)], ps_ref.at[block_rows(i, size)], ps_sem)

        def collect(p, i, size):
            to_partner(p, i, size, 0).wait_recv()
            to_partner(p, i, size, 1).wait_recv()
            stage_partner(i, size).start()

        def halves_sent(p, i, size):
            to_partner(p, i, size, 0).wait_send()
            to_partner(p, i, size, 1).wait_send()

        def first_step(s):
            p = s // 2
            mine = jnp.where(p == 0, 1 - (s + core) % 2, s % 2)
            device = (chip + 2) % chips * CORES + (core + 1 - mine) % 2

            def between():
                @pl.when(s == 0)
                def _():
                    load_wo.wait()
                    load_w2.wait()

                @pl.when((mine == 0) & (p > 0))
                def _():
                    halves_sent(p - 1, p - 1, FIRST)

                @pl.when((mine == 1) & (p > 0))
                def _():
                    collect(p, p, FIRST)

            def after(n):
                @pl.when(mine == 0)
                def _():
                    to_partner(p, p, FIRST, n).start()

            partial(FIRST, device, p, mine, between, after)

            @pl.when(mine == 1)
            def _():
                @pl.when(p == 0)
                def _():
                    collect(p, p, FIRST)

                stage_partner(p, FIRST).wait()
                add(FIRST, 0, 0, width)
                spill(p, FIRST).start()
                spill(p, FIRST).wait()
                to_side(p, 0).start()
                to_side(p, 1).start()

        def later_step(s):
            q = s // 2
            mine = s % 2
            is_mid = q < 2 * blocks
            side = q % 2
            offset = jnp.where(is_mid, 1 + 2 * side, 0)
            block = jnp.where(is_mid, q // 2, q - 2 * blocks)
            device = (chip + offset) % chips * CORES + (core + 1 - mine) % 2
            p = firsts + q
            place = firsts * FIRST // BLOCK + q

            def between():
                @pl.when((mine == 0) & (q == 0))
                def _():
                    halves_sent(firsts - 1, firsts - 1, FIRST)

                @pl.when((mine == 0) & (q > 0))
                def _():
                    halves_sent(p - 1, place - 1, BLOCK)

                @pl.when(mine == 1)
                def _():
                    collect(p, place, BLOCK)

                    @pl.when(is_mid)
                    def _():
                        for k in range(BLOCK // FIRST):
                            b = block * (BLOCK // FIRST) + k
                            part = ro_ref.at[block_rows(side * firsts + b, FIRST)]
                            remote(part, part, recv_o.at[side, b], recv_o.at[side, b], partner).wait_recv()
                        stage_side(side, block).start()

            def after(n):
                @pl.when(mine == 0)
                def _():
                    to_partner(p, place, BLOCK, n).start()

            partial(BLOCK, device, block, mine, between, after)

            @pl.when(mine == 1)
            def _():
                stage_partner(place, BLOCK).wait()
                add(BLOCK, 0, 0, width)

                @pl.when(is_mid)
                def _():
                    stage_side(side, block).wait()
                    add(BLOCK, side * half, 1, half)
                    spill(place, BLOCK).start()
                    spill(place, BLOCK).wait()
                    each(slices, lambda k: to_owner(q, k).start())

                @pl.when(jnp.logical_not(is_mid))
                def _():
                    def final(k):
                        i = block * slices + k
                        rows = block_rows(i, PIECE)
                        load_x = pltpu.make_async_copy(x_ref.at[rows], x_v, xr_sem)
                        load_x.start()
                        copies = []
                        for sd in range(2):
                            src, sem = rn_ref.at[block_rows(sd * blocks * slices + i, PIECE)], recv_n.at[sd, i]
                            remote(src, src, sem, sem, partner).wait_recv()
                            copy = pltpu.make_async_copy(src, stage.at[sd, pl.ds(0, PIECE)], st_sem.at[sd])
                            copy.start()
                            copies.append(copy)
                        load_x.wait()
                        for copy in copies:
                            copy.wait()

                        def finish(n):
                            cols = pl.ds(pl.multiple_of(n * LANES, LANES), LANES)
                            part = pl.ds(0, PIECE)
                            summed = acc[1, block_rows(k, PIECE), cols] + stage[0, part, cols] + stage[1, part, cols]
                            y_v[:, cols] = (x_v[:, cols].astype(f32) + summed).astype(bf16)

                        each(width // LANES, finish)
                        store = pltpu.make_async_copy(y_v, y_ref.at[rows], y_sem)
                        store.start()
                        store.wait()

                    each(slices, final)

        each(2 * firsts, first_step)
        each(2 * blocks * (chips - 1), later_step)
        last = blocks * (chips - 1) - 1
        halves_sent(firsts + last, firsts * FIRST // BLOCK + last, BLOCK)

        def finish_side(b):
            to_side(b, 0).wait_send()
            to_side(b, 1).wait_send()

        each(firsts, finish_side)
        each(2 * blocks, lambda q: each(slices, lambda k: to_owner(q, k).wait_send()))

    ff_width = w1_ref.shape[0]
    pl.run_scoped(
        project_phase,
        pltpu.VMEM((width, heads * qkv_head), bf16),
        pltpu.VMEM(w1_ref.shape, bf16),
        pltpu.VMEM((2, REPACK, heads, qkv_head), bf16),
        pltpu.VMEM((2, GROUP, width), bf16),
        pltpu.VMEM((2, GROUP, ff_width), bf16),
    )
    pl.run_scoped(
        attend_phase,
        pltpu.VMEM((BLOCK, qkv_v.shape[0]), f32),
        pltpu.VMEM((BLOCK, wo_v.shape[0]), bf16),
        pltpu.VMEM((BLOCK, ff_width), bf16),
        pltpu.VMEM((2, BLOCK, width), f32),
        pltpu.VMEM((2, BLOCK, width), f32),
        pltpu.VMEM((PIECE, width), bf16),
        pltpu.VMEM((PIECE, width), bf16),
    )


def transformer_block(chips, x_loc, ln_gamma, w_qkv, w_out, w_up_t, w_down):
    chunk, width = x_loc.shape
    tokens = chunk * chips * CORES
    heads, qkv_head = w_qkv.shape[1], w_qkv.shape[2]
    ff_width = w_up_t.shape[0]
    arrivals = chunk // PIECE + chunk // PIECE // 2
    firsts = chunk // FIRST
    pieces = chunk // PIECE
    pairs = firsts + (chips - 1) * (chunk // BLOCK)
    per_group = GROUP // PIECE
    bf16, f32 = jnp.bfloat16, jnp.float32
    dma = pltpu.SemaphoreType.DMA
    out = pl.pallas_call(
        functools.partial(block_kernel, chips),
        in_specs=[ANY] * 6,
        out_specs=[ANY] * 7,
        out_shape=[
            jax.ShapeDtypeStruct((chunk, width), bf16),
            jax.ShapeDtypeStruct((tokens, width), bf16),
            jax.ShapeDtypeStruct((tokens, ff_width), bf16),
            jax.ShapeDtypeStruct((chips * chunk, width), f32),
            jax.ShapeDtypeStruct((2 * chunk, width // 2), f32),
            jax.ShapeDtypeStruct((2 * chunk, width), f32),
            jax.ShapeDtypeStruct((3 * chunk, width), f32),
        ],
        scratch_shapes=[
            pltpu.VMEM((tokens, heads * qkv_head), bf16),
            pltpu.VMEM(w_out.shape, bf16),
            pltpu.VMEM(w_down.shape, bf16),
            pltpu.VMEM((1, width), f32),
            dma((4,)), dma((chunk // GROUP,)), dma((2,)), dma((2, per_group)), dma((2, per_group)),
            dma((arrivals,)), dma((arrivals,)), dma((arrivals,)), dma((arrivals,)),
            dma((2 * arrivals + 1,)), dma((2 * arrivals + 1,)),
            dma, dma((2,)), dma, dma, dma,
            dma((pairs, 2)), dma((pairs, 2)),
            dma((2, firsts)), dma((2, firsts)),
            dma((2, pieces)), dma((2, pieces)),
        ],
        compiler_params=pltpu.CompilerParams(collective_id=0, has_side_effects=True, vmem_limit_bytes=VMEM_LIMIT),
        name="transformer_block",
    )(x_loc, ln_gamma.reshape(1, width), w_qkv, w_out, w_up_t, w_down)
    return out[0]


def solution(mesh):
    chips = mesh.shape["tp"] // CORES

    def local_block(x_loc, ln_gamma, w_qkv, w_out, w_up, w_down):
        heads, head_dim, model_dim = w_out.shape
        return transformer_block(chips, x_loc, ln_gamma, w_qkv, w_out.reshape(heads * head_dim, model_dim), w_up.T, w_down)

    row_spec = P(("data", "tp"), None)
    return jax.shard_map(local_block, mesh=mesh, in_specs=(row_spec, P(None), P(None, "tp", None), P("tp", None, None), P(None, "tp"), P("tp", None)), out_specs=row_spec, check_vma=False)
```

time: 1030 us -> 474 us (0.46)
  waiting for transfers between devices: 481 us -> 0 us
  Pallas kernels: 0 us -> 467 us
  matrix products: 419 us -> 0 us
  other arithmetic: 104 us -> 0 us
  between operations: 13.9 us -> 0.01 us
    pallas_call x0 -> x1, Pallas kernels: none -> 467 us  [transformer_block(): pl.pallas_call(functools.partial(block_kernel, chips), in_specs=[ANY] * 6...]
    dot_general x12 -> x0, matrix products: 419 us -> none  [the longest x4 105 us: one_block(): jnp.einsum('qhe,khe->hqk', query_blk, key_rows, preferred_element_type=jn...]
    reduce_scatter x1 -> x0, waiting for transfers between devices: 325 us -> none  [local_block(): reduced = lax.psum_scatter(part_sum, 'tp', scatter_dimension=0, tiled=True)]
    all_gather x1 -> x0, waiting for transfers between devices: 156 us -> none  [local_block(): gathered = lax.all_gather(normed, 'tp', axis=0, tiled=True)]
    reduce_sum x6 -> x0, other arithmetic: 91.3 us -> none  [the longest x4 84.9 us: one_block(): exp_sum = jnp.sum(exp_scores, axis=-1, keepdims=True)]
    convert_element_type x2 -> x0, other arithmetic: 13 us -> none  [the longest x1 8 us: local_block(): return (residual + reduced).astype(jnp.bfloat16)]
  transfers between devices with their start and end apart: 2 -> 0, of which waited for: 2 -> 0; matrix products, arithmetic and copies ran while one was open for 0% -> 0% of each run, Pallas kernels for 0% -> 0%
where the time goes in v2:
time: 474 us; the launch traced here: 471 us
  Pallas kernels  467 us (99%)
    pallas_call x1, Pallas kernels, transformer_block(): pl.pallas_call(functools.partial(block_kernel, chips), in_specs=[ANY] * 6...  467 us

profile of v2, /device:TPU:112, one launch (start us, length us, event | category | flops | bytes accessed | tf_op | source)
XLA Modules:
  0.0 471.5 jit_solution(8040359285163042399)
XLA Ops:
  0.0 466.7 %transformer_block.1 = (bf16[512,4096]{1,0:T(8,128)(2,1)}, bf16[4096,4096]{1,0:T(8,128)(2,1)}, bf16[4096,1376]{1,0:T(8,128)(2,1)}, f32[2048,4096]{1,0:T(8,128)},...) custom-call(bf16[512,4096]{1,0:T(8,128)(2,1)} %x_ref.1, f32[1,4096]{1,0:T(1,128)} %bitcast.5, ...), custom_call_target="tpu_custom_call" | custom-call | tf_op jit(solution)/shard_map/transformer_block/pallas_call | solution.py:551
  466.8 4.7 copy.8

commit v3 on v0

v3 whole, which is shorter than its diff:
```python
import functools
import math

import jax
import jax.numpy as jnp
from jax import lax
from jax.experimental import pallas as pl
from jax.experimental.pallas import tpu as pltpu
from jax.sharding import PartitionSpec as P

LN_EPS = 1e-6
MESH = pl.DeviceIdType.MESH
CORES = 2
PIECE = 64
GROUP = 256
BLOCK = 128
FIRST = 64
HELD = 2
REPACK = 256
LATE = 3
COLS = 2048
LANES = 512
VMEM_LIMIT = 67_000_000
ANY = pl.BlockSpec(memory_space=pl.ANY)


def neighbours(chips):
    me = lax.axis_index("tp")
    chip, core = me // CORES, me % CORES
    right = (chip + 1) % chips * CORES + core
    left = (chip + chips - 1) % chips * CORES + core
    partner = chip * CORES + (1 - core)
    return me, chip, core, right, left, partner


def greet(devices):
    barrier = pltpu.get_barrier_semaphore()
    for device in devices:
        pl.semaphore_signal(barrier, inc=1, device_id={"tp": device}, device_id_type=MESH)
    pl.semaphore_wait(barrier, len(devices))


def remote(src, dst, send_sem, recv_sem, device):
    return pltpu.make_async_remote_copy(
        src_ref=src, dst_ref=dst, send_sem=send_sem, recv_sem=recv_sem, device_id={"tp": device}, device_id_type=MESH
    )


def each(count, body):
    def step(i, carry):
        body(i)
        return carry

    lax.fori_loop(0, count, step, 0)


def block_kernel(
    chips, x_ref, gamma_ref, wq_ref, wo_ref, w1_ref, w2_ref,
    y_ref, xg_ref, h_ref, rp_ref, ro_ref, rn_ref, ps_ref,
    qkv_v, wo_v, w2_v, w1_v, lhs, ho, gamma_v,
    w_sem, x_sem, wq_sem, lhs_sem, ho_sem, send_r, recv_l, send_l, recv_r, send_g, recv_g,
    h_sem, st_sem, xr_sem, y_sem, ps_sem, send_p, recv_p, send_o, recv_o, send_n, recv_n,
):
    me, chip, core, right, left, partner = neighbours(chips)
    chunk, width = x_ref.shape
    heads, qkv_head = wq_ref.shape[1], wq_ref.shape[2]
    load_wo = pltpu.make_async_copy(wo_ref, wo_v, w_sem.at[1])
    load_w2 = pltpu.make_async_copy(w2_ref, w2_v, w_sem.at[2])
    bf16, f32 = jnp.bfloat16, jnp.float32

    own_pieces = chunk // PIECE
    half = own_pieces // 2
    arrivals = own_pieces + half
    per_group = GROUP // PIECE
    own_groups = chunk // GROUP
    first = own_groups * CORES
    groups = first + arrivals

    def load_x(piece):
        slot, row = piece // per_group, piece % per_group * PIECE
        return pltpu.make_async_copy(x_ref.at[pl.ds(piece * PIECE, PIECE)], lhs.at[slot, pl.ds(row, PIECE)], x_sem.at[piece])

    for j in range(half):
        load_x(j).start()
        load_x(j + half).start()
    load_gamma = pltpu.make_async_copy(gamma_ref, gamma_v, w_sem.at[3])
    load_gamma.start()

    load_w1 = pltpu.make_async_copy(w1_ref, w1_v, w_sem.at[0])
    greet((right, left, partner))

    def rows_at(device, piece):
        return pl.ds(pl.multiple_of(device * chunk + piece * PIECE, PIECE), PIECE)

    def own_send(piece, sends, recvs, j, device):
        rows = xg_ref.at[rows_at(me, piece)]
        return remote(rows, rows, sends.at[j], recvs.at[j], device)

    def to_right(j):
        return own_send(j, send_r, recv_l, j, right)

    def to_left(j):
        return own_send((j + half) % own_pieces, send_l, recv_r, j, left)

    def own_to_partner():
        rows = xg_ref.at[pl.ds(pl.multiple_of(me * chunk, chunk), chunk)]
        return remote(rows, rows, send_g.at[2 * arrivals], recv_g.at[2 * arrivals], partner)

    def normalise(j):
        out = []
        for side in range(2):
            rows = pl.ds(j * PIECE, PIECE)
            piece = j + side * half
            load_x(piece).wait()
            vals = lhs[side, rows, :].astype(f32)
            centered = vals - jnp.mean(vals, axis=-1, keepdims=True)
            var = jnp.mean(centered * centered, axis=-1, keepdims=True)
            lhs[side, rows, :] = (centered * lax.rsqrt(var + LN_EPS) * gamma_v[...]).astype(bf16)
            copy = pltpu.make_async_copy(lhs.at[side, rows], xg_ref.at[rows_at(me, piece)], lhs_sem.at[side, 0])
            copy.start()
            out.append(copy)
        for copy in out:
            copy.wait()

    def left_row(j, c):
        return ((chip + chips - 1 - j // own_pieces) % chips * CORES + c) * chunk + j % own_pieces * PIECE

    def right_row(j, c):
        return ((chip + 1 + j // own_pieces) % chips * CORES + c) * chunk + (j + half) % own_pieces * PIECE

    def side_rows(j, side, c):
        row = right_row(j, c) if side else left_row(j, c)
        return pl.ds(pl.multiple_of(row, PIECE), PIECE)

    def lhs_copy(src, slot, i):
        return pltpu.make_async_copy(src, lhs.at[slot, pl.ds(i * PIECE, PIECE)], lhs_sem.at[slot, i])

    def relay(j, side):
        rows = xg_ref.at[side_rows(j, side, core)]
        sends, recvs, device = (send_l, recv_r, left) if side else (send_r, recv_l, right)
        return remote(rows, rows, sends.at[own_pieces + j], recvs.at[own_pieces + j], device)

    def share(j, side, c):
        rows = xg_ref.at[side_rows(j, side, c)]
        return remote(rows, rows, send_g.at[2 * j + side], recv_g.at[2 * j + side], partner)

    def fetch_links(g):
        slot = g % 2

        @pl.when((g >= own_groups) & (g < first))
        def _():
            @pl.when(g == own_groups)
            def _():
                own_to_partner().wait_recv()

            for i in range(per_group):
                lhs_copy(xg_ref.at[rows_at(partner, (g - own_groups) * per_group + i)], slot, i).start()

        @pl.when(g >= first)
        def _():
            j = g - first
            for side in range(2):
                rows = xg_ref.at[side_rows(j, side, core)]
                sem = (recv_r if side else recv_l).at[j]
                remote(rows, rows, sem, sem, partner).wait_recv()

            @pl.when(j < half)
            def _():
                relay(j, 0).start()
                relay(j, 1).start()

            for side in range(2):
                share(j, side, core).start()
                lhs_copy(xg_ref.at[side_rows(j, side, core)], slot, side).start()

    def fetch_partner(g):
        @pl.when(g >= first)
        def _():
            j = g - first
            for side in range(2):
                share(j, side, 1 - core).wait_recv()
            for side in range(2):
                lhs_copy(xg_ref.at[side_rows(j, side, 1 - core)], g % 2, 2 + side).start()

    def group_row(g, i):
        j = g - first
        early = jnp.where(g < own_groups, me, partner) * chunk + ((g % own_groups) * per_group + i) * PIECE
        c = core if i < 2 else 1 - core
        late = right_row(j, c) if i % 2 else left_row(j, c)
        return pl.ds(pl.multiple_of(jnp.where(g < first, early, late), PIECE), PIECE)

    def out_copy(g, i):
        slot = g % 2
        return pltpu.make_async_copy(ho.at[slot, pl.ds(i * PIECE, PIECE)], h_ref.at[group_row(g, i)], ho_sem.at[slot, i])

    def wait_out(g):
        for i in range(per_group):
            out_copy(g, i).wait()

    def compute_up(g):
        slot = g % 2

        @pl.when((g >= 2) & (g < groups - HELD))
        def _():
            wait_out(g - 2)

        pre = lax.dot_general(lhs[slot], w1_v[...], (((1,), (1,)), ((), ())), preferred_element_type=f32)
        ho[slot] = jax.nn.gelu(pre, approximate=True).astype(bf16)
        for i in range(per_group):
            out_copy(g, i).start()

    def finish_gather():
        own_to_partner().wait_send()

        def finish_own(j):
            to_right(j).wait_send()
            to_left(j).wait_send()

        def finish_relay(j):
            relay(j, 0).wait_send()
            relay(j, 1).wait_send()

        def finish_share(j):
            share(j, 0, core).wait_send()
            share(j, 1, core).wait_send()

        each(own_pieces, finish_own)
        each(half, finish_relay)
        each(arrivals, finish_share)

    def project_phase(wq_v, w4_v):
        def load_wq(i):
            rows = pl.ds(pl.multiple_of(i * REPACK, REPACK), REPACK)
            return pltpu.make_async_copy(wq_ref.at[rows], w4_v.at[i % 2], wq_sem.at[i % 2])

        load_wq(0).start()
        load_w1.start()
        load_gamma.wait()
        for j in range(half):
            normalise(j)
            to_right(j).start()
            to_left(j).start()
        own_to_partner().start()

        def open_rest(j):
            to_right(half + j).start()
            to_left(half + j).start()

        each(half, open_rest)
        load_wo.start()
        load_w2.start()

        def repack(i):
            @pl.when(i < width // REPACK - 1)
            def _():
                load_wq(i + 1).start()

            load_wq(i).wait()
            rows = pl.ds(pl.multiple_of(i * REPACK, REPACK), REPACK)
            wq_v[rows, :] = w4_v[i % 2].reshape(REPACK, heads * qkv_head)

        each(width // REPACK, repack)
        load_w1.wait()

        def compute_qkv(g):
            slot = g % 2

            @pl.when(g >= own_groups)
            def _():
                for i in range(per_group):
                    lhs_copy(xg_ref.at[rows_at(me, i)], slot, i).wait()

            tile = jnp.dot(lhs[slot], wq_v[...], preferred_element_type=f32).astype(bf16)
            for i in range(per_group):
                qkv_v[group_row(g, i), :] = tile[i * PIECE:(i + 1) * PIECE]

        def step(g):
            ahead = g < groups - LATE

            @pl.when(ahead)
            def _():
                fetch_links(g + 1)

            compute_qkv(g)

            @pl.when(ahead)
            def _():
                fetch_partner(g + 1)

            @pl.when(g < groups - HELD)
            def _():
                compute_up(g)

            @pl.when(jnp.logical_not(ahead) & (g < groups - 1))
            def _():
                fetch_links(g + 1)
                fetch_partner(g + 1)

        each(groups, step)
        for g in range(groups - HELD - 2, groups - HELD):
            wait_out(jnp.int32(g))

    def attend_phase(s_v, o_v, h_v, away, acc, stage, stage_half, x_v, y_v):
        head_dim = qkv_head // 3
        firsts = chunk // FIRST
        blocks = chunk // BLOCK
        cols_half = width // 2
        slices = BLOCK // PIECE
        factor = head_dim ** -0.5 * math.log2(math.e)

        def block_rows(i, size):
            return pl.ds(pl.multiple_of(i * size, size), size)

        def to_partner(p, i, size, side):
            cols = pl.ds(side * cols_half, cols_half)
            src = away.at[pl.ds(0, size), cols]
            dst = rp_ref.at[block_rows(i, size), cols]
            return remote(src, dst, send_p.at[p, side], recv_p.at[p, side], partner)

        def to_side(b, side):
            src = ps_ref.at[block_rows(b, FIRST), pl.ds(side * cols_half, cols_half)]
            dst = ro_ref.at[block_rows(side * firsts + b, FIRST)]
            return remote(src, dst, send_o.at[side, b], recv_o.at[side, b], left if side else right)

        def to_owner(q, k):
            side, block = q % 2, q // 2
            i = block * slices + k
            src = ps_ref.at[block_rows(firsts * FIRST // PIECE + q * slices + k, PIECE)]
            dst = rn_ref.at[block_rows(side * blocks * slices + i, PIECE)]
            device = (chip + 1 + 2 * side) % chips * CORES + core
            return remote(src, dst, send_n.at[side, i], recv_n.at[side, i], device)

        def attend_head(size, rows, head):
            base = pl.multiple_of(head * qkv_head, head_dim)
            q = jnp.concatenate([qkv_v[row, pl.ds(base, head_dim)] for row in rows], axis=0)
            k_cols = pl.ds(pl.multiple_of(base + head_dim, head_dim), head_dim)
            v_cols = pl.ds(pl.multiple_of(base + 2 * head_dim, head_dim), head_dim)
            part = pl.ds(0, 2 * size)
            s = lax.dot_general(q, qkv_v[:, k_cols], (((1,), (1,)), ((), ())), preferred_element_type=f32)
            s_v[part, :] = s
            top = jnp.max(s, axis=-1, keepdims=True)
            e = jnp.exp2((s_v[part, :] - top) * factor)
            total = jnp.sum(e, axis=-1, keepdims=True)
            out = jnp.dot(e.astype(bf16), qkv_v[:, v_cols], preferred_element_type=f32)
            o_v[part, pl.ds(pl.multiple_of(head * head_dim, head_dim), head_dim)] = (out / total).astype(bf16)

        def stage_partner(i, size):
            return pltpu.make_async_copy(rp_ref.at[block_rows(i, size)], stage.at[pl.ds(0, size)], st_sem.at[0])

        def stage_side(side, block):
            src = ro_ref.at[block_rows(side * blocks + block, BLOCK)]
            return pltpu.make_async_copy(src, stage_half, st_sem.at[1])

        def add(size, slot, base, addend):
            def tile(n):
                dst = pl.ds(pl.multiple_of(base + n * LANES, LANES), LANES)
                src = pl.ds(pl.multiple_of(n * LANES, LANES), LANES)
                acc[slot, pl.ds(0, size), dst] += addend[pl.ds(0, size), src]

            each(addend.shape[1] // LANES, tile)

        def spill(slot, i, size):
            return pltpu.make_async_copy(acc.at[slot, pl.ds(0, size)], ps_ref.at[block_rows(i, size)], ps_sem)

        def collect(p, i, size):
            to_partner(p, i, size, 0).wait_recv()
            to_partner(p, i, size, 1).wait_recv()
            stage_partner(i, size).start()

        def sent(p, i, size):
            to_partner(p, i, size, 0).wait_send()
            to_partner(p, i, size, 1).wait_send()

        def partial(size, p, i, chip_offset, block, between):
            base = (chip + chip_offset) % chips * CORES
            rows = [block_rows((base + c) * (chunk // size) + block, size) for c in (1 - core, core)]
            loads = [
                pltpu.make_async_copy(h_ref.at[row], h_v.at[pl.ds(n * size, size)], h_sem.at[n])
                for n, row in enumerate(rows)
            ]
            for load in loads:
                load.start()
            each(heads, lambda head: attend_head(size, rows, head))
            for load in loads:
                load.wait()
            between()
            part = pl.ds(0, 2 * size)
            for n in range(width // COLS):
                cols = pl.ds(n * COLS, COLS)
                both = jnp.dot(
                    o_v[part, :], wo_v[:, cols], preferred_element_type=f32
                ) + jnp.dot(h_v[part, :], w2_v[:, cols], preferred_element_type=f32)
                away[pl.ds(0, size), cols] = both[:size]
                acc[p % 2, pl.ds(0, size), cols] = both[size:]
                to_partner(p, i, size, n).start()

        def first_collect(s):
            collect(s, s, FIRST)

        def first_finish(s):
            slot = s % 2
            stage_partner(s, FIRST).wait()
            add(FIRST, slot, 0, stage)
            spill(slot, s, FIRST).start()
            spill(slot, s, FIRST).wait()
            to_side(s, 0).start()
            to_side(s, 1).start()

        def first_step(s):
            def between():
                @pl.when(s == 0)
                def _():
                    load_wo.wait()
                    load_w2.wait()

                @pl.when(s > 0)
                def _():
                    sent(s - 1, s - 1, FIRST)

                @pl.when(s > HELD)
                def _():
                    first_collect(s - 1)

            partial(FIRST, s, s, 2, s, between)

            @pl.when(s < HELD)
            def _():
                compute_up(groups - HELD + s)
                first_collect(s)
                first_finish(s)

            @pl.when(s == HELD - 1)
            def _():
                for g in range(groups - HELD, groups):
                    wait_out(jnp.int32(g))

            @pl.when(s > HELD)
            def _():
                first_finish(s - 1)

        skip = firsts * FIRST // BLOCK

        def later_parts(q):
            is_mid = q < 2 * blocks
            return is_mid, q % 2, jnp.where(is_mid, q // 2, q - 2 * blocks)

        def later_collect(q):
            is_mid, side, block = later_parts(q)
            collect(firsts + q, skip + q, BLOCK)

            @pl.when(is_mid)
            def _():
                for k in range(BLOCK // FIRST):
                    b = block * (BLOCK // FIRST) + k
                    part = ro_ref.at[block_rows(side * firsts + b, FIRST)]
                    remote(part, part, recv_o.at[side, b], recv_o.at[side, b], partner).wait_recv()
                stage_side(side, block).start()

        def later_finish(q):
            is_mid, side, block = later_parts(q)
            slot = (firsts + q) % 2
            stage_partner(skip + q, BLOCK).wait()
            add(BLOCK, slot, 0, stage)

            @pl.when(is_mid)
            def _():
                stage_side(side, block).wait()
                add(BLOCK, slot, side * cols_half, stage_half)
                spill(slot, skip + q, BLOCK).start()
                spill(slot, skip + q, BLOCK).wait()
                each(slices, lambda k: to_owner(q, k).start())

            @pl.when(jnp.logical_not(is_mid))
            def _():
                def final(k):
                    i = block * slices + k
                    rows = block_rows(i, PIECE)
                    load = pltpu.make_async_copy(x_ref.at[rows], x_v, xr_sem)
                    load.start()
                    copies = []
                    for sd in range(2):
                        src, sem = rn_ref.at[block_rows(sd * blocks * slices + i, PIECE)], recv_n.at[sd, i]
                        remote(src, src, sem, sem, partner).wait_recv()
                        copy = pltpu.make_async_copy(src, stage.at[pl.ds(sd * PIECE, PIECE)], st_sem.at[sd])
                        copy.start()
                        copies.append(copy)
                    load.wait()
                    for copy in copies:
                        copy.wait()

                    def tile(n):
                        cols = pl.ds(pl.multiple_of(n * LANES, LANES), LANES)
                        mine = acc[slot, block_rows(k, PIECE), cols]
                        summed = mine + stage[0:PIECE, cols] + stage[PIECE:2 * PIECE, cols]
                        y_v[:, cols] = (x_v[:, cols].astype(f32) + summed).astype(bf16)

                    each(width // LANES, tile)
                    store = pltpu.make_async_copy(y_v, y_ref.at[rows], y_sem)
                    store.start()
                    store.wait()

                each(slices, final)

        def later_step(q):
            is_mid, side, block = later_parts(q)
            p = firsts + q

            def between():
                @pl.when(q == 0)
                def _():
                    sent(firsts - 1, firsts - 1, FIRST)

                @pl.when(q > 0)
                def _():
                    sent(p - 1, skip + q - 1, BLOCK)
                    later_collect(q - 1)

            partial(BLOCK, p, skip + q, jnp.where(is_mid, 1 + 2 * side, 0), block, between)

            @pl.when(q > 0)
            def _():
                later_finish(q - 1)

        later = blocks * (chips - 1)
        each(firsts, first_step)
        first_collect(jnp.int32(firsts - 1))
        first_finish(jnp.int32(firsts - 1))
        each(later, later_step)
        later_collect(jnp.int32(later - 1))
        later_finish(jnp.int32(later - 1))
        sent(jnp.int32(firsts + later - 1), jnp.int32(skip + later - 1), BLOCK)

        def finish_side(b):
            to_side(b, 0).wait_send()
            to_side(b, 1).wait_send()

        each(firsts, finish_side)
        each(2 * blocks, lambda q: each(slices, lambda k: to_owner(q, k).wait_send()))

    pl.run_scoped(
        project_phase,
        pltpu.VMEM((width, heads * qkv_head), bf16),
        pltpu.VMEM((2, REPACK, heads, qkv_head), bf16),
    )
    pl.run_scoped(
        attend_phase,
        pltpu.VMEM((2 * BLOCK, qkv_v.shape[0]), f32),
        pltpu.VMEM((2 * BLOCK, wo_v.shape[0]), bf16),
        pltpu.VMEM((2 * BLOCK, h_ref.shape[1]), bf16),
        pltpu.VMEM((BLOCK, width), f32),
        pltpu.VMEM((2, BLOCK, width), f32),
        pltpu.VMEM((BLOCK, width), f32),
        pltpu.VMEM((BLOCK, width // 2), f32),
        pltpu.VMEM((PIECE, width), bf16),
        pltpu.VMEM((PIECE, width), bf16),
    )
    finish_gather()


def transformer_block(chips, x_loc, ln_gamma, w_qkv, w_out, w_up_t, w_down):
    chunk, width = x_loc.shape
    tokens = chunk * chips * CORES
    heads, qkv_head = w_qkv.shape[1], w_qkv.shape[2]
    ff_width = w_up_t.shape[0]
    arrivals = chunk // PIECE + chunk // PIECE // 2
    firsts = chunk // FIRST
    pieces = chunk // PIECE
    pairs = firsts + (chips - 1) * (chunk // BLOCK)
    per_group = GROUP // PIECE
    bf16, f32 = jnp.bfloat16, jnp.float32
    dma = pltpu.SemaphoreType.DMA
    out = pl.pallas_call(
        functools.partial(block_kernel, chips),
        in_specs=[ANY] * 6,
        out_specs=[ANY] * 7,
        out_shape=[
            jax.ShapeDtypeStruct((chunk, width), bf16),
            jax.ShapeDtypeStruct((tokens, width), bf16),
            jax.ShapeDtypeStruct((tokens, ff_width), bf16),
            jax.ShapeDtypeStruct((chips * chunk, width), f32),
            jax.ShapeDtypeStruct((2 * chunk, width // 2), f32),
            jax.ShapeDtypeStruct((2 * chunk, width), f32),
            jax.ShapeDtypeStruct((3 * chunk, width), f32),
        ],
        scratch_shapes=[
            pltpu.VMEM((tokens, heads * qkv_head), bf16),
            pltpu.VMEM(w_out.shape, bf16),
            pltpu.VMEM(w_down.shape, bf16),
            pltpu.VMEM(w_up_t.shape, bf16),
            pltpu.VMEM((2, GROUP, width), bf16),
            pltpu.VMEM((2, GROUP, ff_width), bf16),
            pltpu.VMEM((1, width), f32),
            dma((4,)), dma((pieces,)), dma((2,)), dma((2, per_group)), dma((2, per_group)),
            dma((arrivals,)), dma((arrivals,)), dma((arrivals,)), dma((arrivals,)),
            dma((2 * arrivals + 1,)), dma((2 * arrivals + 1,)),
            dma((2,)), dma((2,)), dma, dma, dma,
            dma((pairs, 2)), dma((pairs, 2)),
            dma((2, firsts)), dma((2, firsts)),
            dma((2, pieces)), dma((2, pieces)),
        ],
        compiler_params=pltpu.CompilerParams(collective_id=0, has_side_effects=True, vmem_limit_bytes=VMEM_LIMIT),
        name="transformer_block",
    )(x_loc, ln_gamma.reshape(1, width), w_qkv, w_out, w_up_t, w_down)
    return out[0]


def solution(mesh):
    chips = mesh.shape["tp"] // CORES

    def local_block(x_loc, ln_gamma, w_qkv, w_out, w_up, w_down):
        heads, head_dim, model_dim = w_out.shape
        return transformer_block(chips, x_loc, ln_gamma, w_qkv, w_out.reshape(heads * head_dim, model_dim), w_up.T, w_down)

    row_spec = P(("data", "tp"), None)
    return jax.shard_map(local_block, mesh=mesh, in_specs=(row_spec, P(None), P(None, "tp", None), P("tp", None, None), P(None, "tp"), P("tp", None)), out_specs=row_spec, check_vma=False)
```

time: 1030 us -> 460 us (0.45)
  waiting for transfers between devices: 481 us -> 0 us
  Pallas kernels: 0 us -> 454 us
  matrix products: 419 us -> 0 us
  other arithmetic: 104 us -> 0 us
  between operations: 13.9 us -> 0.01 us
    pallas_call x0 -> x1, Pallas kernels: none -> 454 us  [transformer_block(): pl.pallas_call(functools.partial(block_kernel, chips), in_specs=[ANY] * 6...]
    dot_general x12 -> x0, matrix products: 419 us -> none  [the longest x4 105 us: one_block(): jnp.einsum('qhe,khe->hqk', query_blk, key_rows, preferred_element_type=jn...]
    reduce_scatter x1 -> x0, waiting for transfers between devices: 325 us -> none  [local_block(): reduced = lax.psum_scatter(part_sum, 'tp', scatter_dimension=0, tiled=True)]
    all_gather x1 -> x0, waiting for transfers between devices: 156 us -> none  [local_block(): gathered = lax.all_gather(normed, 'tp', axis=0, tiled=True)]
    reduce_sum x6 -> x0, other arithmetic: 91.3 us -> none  [the longest x4 84.9 us: one_block(): exp_sum = jnp.sum(exp_scores, axis=-1, keepdims=True)]
    convert_element_type x2 -> x0, other arithmetic: 13 us -> none  [the longest x1 8 us: local_block(): return (residual + reduced).astype(jnp.bfloat16)]
  transfers between devices with their start and end apart: 2 -> 0, of which waited for: 2 -> 0; matrix products, arithmetic and copies ran while one was open for 0% -> 0% of each run, Pallas kernels for 0% -> 0%
where the time goes in v3:
time: 460 us; the launch traced here: 459 us
  Pallas kernels  454 us (99%)
  local copies, waits for them, and re-layouts  4.7 us (1%)
    pallas_call x1, Pallas kernels, transformer_block(): pl.pallas_call(functools.partial(block_kernel, chips), in_specs=[ANY] * 6...  454 us

profile of v3, /device:TPU:112, one launch (start us, length us, event | category | flops | bytes accessed | tf_op | source)
XLA Modules:
  0.0 458.9 jit_solution(13184775526677206655)
XLA Ops:
  0.0 454.2 %transformer_block.1 = (bf16[512,4096]{1,0:T(8,128)(2,1)}, bf16[4096,4096]{1,0:T(8,128)(2,1)}, bf16[4096,1376]{1,0:T(8,128)(2,1)}, f32[2048,4096]{1,0:T(8,128)},...) custom-call(bf16[512,4096]{1,0:T(8,128)(2,1)} %x_ref.1, f32[1,4096]{1,0:T(1,128)} %bitcast.5, ...), custom_call_target="tpu_custom_call" | custom-call | tf_op jit(solution)/shard_map/transformer_block/pallas_call | solution.py:572
  454.2 4.7 %copy.8 = bf16[512,4096]{1,0:T(8,128)(2,1)} copy(bf16[512,4096]{1,0:T(8,128)(2,1)} %get-tuple-element.6) | data formatting | bytes 8388608

commit v4 on v3

--- a/solution.py
+++ b/solution.py
@@ -15,7 +15,7 @@
 GROUP = 256
 BLOCK = 128
 FIRST = 64
-HELD = 2
+HELD = 1
 REPACK = 256
 LATE = 3
 COLS = 2048
@@ -371,7 +371,7 @@
             to_partner(p, i, size, 0).wait_send()
             to_partner(p, i, size, 1).wait_send()
 
-        def partial(size, p, i, chip_offset, block, between):
+        def partial(size, p, i, chip_offset, block, late, between, flush):
             base = (chip + chip_offset) % chips * CORES
             rows = [block_rows((base + c) * (chunk // size) + block, size) for c in (1 - core, core)]
             loads = [
@@ -380,7 +380,12 @@
             ]
             for load in loads:
                 load.start()
-            each(heads, lambda head: attend_head(size, rows, head))
+
+            def one_head(head):
+                pl.when(head == heads - 1)(late)
+                attend_head(size, rows, head)
+
+            each(heads, one_head)
             for load in loads:
                 load.wait()
             between()
@@ -393,50 +398,55 @@
                 away[pl.ds(0, size), cols] = both[:size]
                 acc[p % 2, pl.ds(0, size), cols] = both[size:]
                 to_partner(p, i, size, n).start()
+                if n == 0:
+                    flush()
 
         def first_collect(s):
             collect(s, s, FIRST)
 
-        def first_finish(s):
-            slot = s % 2
+        def first_sum(s):
             stage_partner(s, FIRST).wait()
-            add(FIRST, slot, 0, stage)
-            spill(slot, s, FIRST).start()
-            spill(slot, s, FIRST).wait()
+            add(FIRST, s % 2, 0, stage)
+            spill(s % 2, s, FIRST).start()
+
+        def first_send(s):
+            spill(s % 2, s, FIRST).wait()
             to_side(s, 0).start()
             to_side(s, 1).start()
 
         def first_step(s):
+            @pl.when(s == firsts // 4)
+            def _():
+                for g in range(groups - HELD, groups):
+                    compute_up(jnp.int32(g))
+
+            def late():
+                @pl.when(s > 0)
+                def _():
+                    first_collect(s - 1)
+
             def between():
                 @pl.when(s == 0)
                 def _():
                     load_wo.wait()
                     load_w2.wait()
 
+                @pl.when(s == firsts // 4)
+                def _():
+                    for g in range(groups - HELD, groups):
+                        wait_out(jnp.int32(g))
+
                 @pl.when(s > 0)
                 def _():
                     sent(s - 1, s - 1, FIRST)
-
-                @pl.when(s > HELD)
-                def _():
-                    first_collect(s - 1)
-
-            partial(FIRST, s, s, 2, s, between)
-
-            @pl.when(s < HELD)
-            def _():
-                compute_up(groups - HELD + s)
-                first_collect(s)
-                first_finish(s)
-
-            @pl.when(s == HELD - 1)
-            def _():
-                for g in range(groups - HELD, groups):
-                    wait_out(jnp.int32(g))
-
-            @pl.when(s > HELD)
-            def _():
-                first_finish(s - 1)
+                    first_sum(s - 1)
+
+            def flush():
+                @pl.when(s > 0)
+                def _():
+                    first_send(s - 1)
+
+            partial(FIRST, s, s, 2, s, late, between, flush)
 
         skip = firsts * FIRST // BLOCK
 
@@ -456,7 +466,7 @@
                     remote(part, part, recv_o.at[side, b], recv_o.at[side, b], partner).wait_recv()
                 stage_side(side, block).start()
 
-        def later_finish(q):
+        def later_sum(q):
             is_mid, side, block = later_parts(q)
             slot = (firsts + q) % 2
             stage_partner(skip + q, BLOCK).wait()
@@ -467,8 +477,6 @@
                 stage_side(side, block).wait()
                 add(BLOCK, slot, side * cols_half, stage_half)
                 spill(slot, skip + q, BLOCK).start()
-                spill(slot, skip + q, BLOCK).wait()
-                each(slices, lambda k: to_owner(q, k).start())
 
             @pl.when(jnp.logical_not(is_mid))
             def _():
@@ -501,33 +509,52 @@
 
                 each(slices, final)
 
+        def later_send(q):
+            @pl.when(later_parts(q)[0])
+            def _():
+                spill((firsts + q) % 2, skip + q, BLOCK).wait()
+                each(slices, lambda k: to_owner(q, k).start())
+
         def later_step(q):
             is_mid, side, block = later_parts(q)
             p = firsts + q
 
+            def late():
+                @pl.when(q == 0)
+                def _():
+                    first_collect(jnp.int32(firsts - 1))
+
+                @pl.when(q > 0)
+                def _():
+                    later_collect(q - 1)
+
             def between():
                 @pl.when(q == 0)
                 def _():
                     sent(firsts - 1, firsts - 1, FIRST)
+                    first_sum(jnp.int32(firsts - 1))
 
                 @pl.when(q > 0)
                 def _():
                     sent(p - 1, skip + q - 1, BLOCK)
-                    later_collect(q - 1)
-
-            partial(BLOCK, p, skip + q, jnp.where(is_mid, 1 + 2 * side, 0), block, between)
-
-            @pl.when(q > 0)
-            def _():
-                later_finish(q - 1)
+                    later_sum(q - 1)
+
+            def flush():
+                @pl.when(q == 0)
+                def _():
+                    first_send(jnp.int32(firsts - 1))
+
+                @pl.when(q > 0)
+                def _():
+                    later_send(q - 1)
+
+            partial(BLOCK, p, skip + q, jnp.where(is_mid, 1 + 2 * side, 0), block, late, between, flush)
 
         later = blocks * (chips - 1)
         each(firsts, first_step)
-        first_collect(jnp.int32(firsts - 1))
-        first_finish(jnp.int32(firsts - 1))
         each(later, later_step)
         later_collect(jnp.int32(later - 1))
-        later_finish(jnp.int32(later - 1))
+        later_sum(jnp.int32(later - 1))
         sent(jnp.int32(firsts + later - 1), jnp.int32(skip + later - 1), BLOCK)
 
         def finish_side(b):

time: 460 us -> 450 us (0.978)
  Pallas kernels: 454 us -> 444 us
    pallas_call x1, Pallas kernels: 454 us -> 444 us  [transformer_block(): pl.pallas_call(functools.partial(block_kernel, chips), in_specs=[ANY] * 6...]
where the time goes in v4:
time: 450 us; the launch traced here: 448 us
  Pallas kernels  444 us (99%)
  local copies, waits for them, and re-layouts  4.7 us (1%)
    pallas_call x1, Pallas kernels, transformer_block(): pl.pallas_call(functools.partial(block_kernel, chips), in_specs=[ANY] * 6...  444 us

profile of v4, /device:TPU:112, one launch (start us, length us, event | category | flops | bytes accessed | tf_op | source)
XLA Modules:
  0.0 448.3 jit_solution(12175667507704238555)
XLA Ops:
  0.0 443.6 %transformer_block.1 = (bf16[512,4096]{1,0:T(8,128)(2,1)}, bf16[4096,4096]{1,0:T(8,128)(2,1)}, bf16[4096,1376]{1,0:T(8,128)(2,1)}, f32[2048,4096]{1,0:T(8,128)},...) custom-call(bf16[512,4096]{1,0:T(8,128)(2,1)} %x_ref.1, f32[1,4096]{1,0:T(1,128)} %bitcast.5, ...), custom_call_target="tpu_custom_call" | custom-call | tf_op jit(solution)/shard_map/transformer_block/pallas_call | solution.py:599
  443.6 4.7 %copy.8 = bf16[512,4096]{1,0:T(8,128)(2,1)} copy(bf16[512,4096]{1,0:T(8,128)(2,1)} %get-tuple-element.6) | data formatting | bytes 8388608

commit v5 on v4

--- a/solution.py
+++ b/solution.py
@@ -15,9 +15,9 @@
 GROUP = 256
 BLOCK = 128
 FIRST = 64
-HELD = 1
+HELD = 2
 REPACK = 256
-LATE = 3
+LATE = 4
 COLS = 2048
 LANES = 512
 VMEM_LIMIT = 67_000_000
@@ -96,6 +96,12 @@
         rows = xg_ref.at[rows_at(me, piece)]
         return remote(rows, rows, sends.at[j], recvs.at[j], device)
 
+    def opening(side):
+        src = lhs.at[side, pl.ds(0, PIECE)]
+        dst = xg_ref.at[rows_at(me, side * half)]
+        sends, recvs, device = (send_l, recv_r, left) if side else (send_r, recv_l, right)
+        return remote(src, dst, sends.at[0], recvs.at[0], device)
+
     def to_right(j):
         return own_send(j, send_r, recv_l, j, right)
 
@@ -119,6 +125,8 @@
             copy = pltpu.make_async_copy(lhs.at[side, rows], xg_ref.at[rows_at(me, piece)], lhs_sem.at[side, 0])
             copy.start()
             out.append(copy)
+            if j == 0:
+                opening(side).start()
         for copy in out:
             copy.wait()
 
@@ -151,6 +159,8 @@
         def _():
             @pl.when(g == own_groups)
             def _():
+                for side in range(2):
+                    opening(side).wait_send()
                 own_to_partner().wait_recv()
 
             for i in range(per_group):
@@ -213,8 +223,8 @@
         own_to_partner().wait_send()
 
         def finish_own(j):
-            to_right(j).wait_send()
-            to_left(j).wait_send()
+            to_right(j + 1).wait_send()
+            to_left(j + 1).wait_send()
 
         def finish_relay(j):
             relay(j, 0).wait_send()
@@ -224,7 +234,7 @@
             share(j, 0, core).wait_send()
             share(j, 1, core).wait_send()
 
-        each(own_pieces, finish_own)
+        each(own_pieces - 1, finish_own)
         each(half, finish_relay)
         each(arrivals, finish_share)
 
@@ -238,8 +248,9 @@
         load_gamma.wait()
         for j in range(half):
             normalise(j)
-            to_right(j).start()
-            to_left(j).start()
+            if j > 0:
+                to_right(j).start()
+                to_left(j).start()
         own_to_partner().start()
 
         def open_rest(j):
@@ -262,17 +273,18 @@
         each(width // REPACK, repack)
         load_w1.wait()
 
-        def compute_qkv(g):
+        def qkv_rows(g, pieces):
             slot = g % 2
 
             @pl.when(g >= own_groups)
             def _():
-                for i in range(per_group):
+                for i in pieces:
                     lhs_copy(xg_ref.at[rows_at(me, i)], slot, i).wait()
 
-            tile = jnp.dot(lhs[slot], wq_v[...], preferred_element_type=f32).astype(bf16)
-            for i in range(per_group):
-                qkv_v[group_row(g, i), :] = tile[i * PIECE:(i + 1) * PIECE]
+            rows = pl.ds(pieces[0] * PIECE, len(pieces) * PIECE)
+            tile = jnp.dot(lhs[slot, rows, :], wq_v[...], preferred_element_type=f32).astype(bf16)
+            for n, i in enumerate(pieces):
+                qkv_v[group_row(g, i), :] = tile[n * PIECE:(n + 1) * PIECE]
 
         def step(g):
             ahead = g < groups - LATE
@@ -281,7 +293,11 @@
             def _():
                 fetch_links(g + 1)
 
-            compute_qkv(g)
+            qkv_rows(g, range(per_group))
+
+            @pl.when(jnp.logical_not(ahead))
+            def _():
+                fetch_links(g + 1)
 
             @pl.when(ahead)
             def _():
@@ -291,12 +307,15 @@
             def _():
                 compute_up(g)
 
-            @pl.when(jnp.logical_not(ahead) & (g < groups - 1))
-            def _():
-                fetch_links(g + 1)
+            @pl.when(jnp.logical_not(ahead) & (g < groups - 2))
+            def _():
                 fetch_partner(g + 1)
 
-        each(groups, step)
+        each(groups - 1, step)
+        last = jnp.int32(groups - 1)
+        qkv_rows(last, range(per_group // 2))
+        fetch_partner(last)
+        qkv_rows(last, range(per_group // 2, per_group))
         for g in range(groups - HELD - 2, groups - HELD):
             wait_out(jnp.int32(g))
 
@@ -371,18 +390,21 @@
             to_partner(p, i, size, 0).wait_send()
             to_partner(p, i, size, 1).wait_send()
 
-        def partial(size, p, i, chip_offset, block, late, between, flush):
+        def partial(size, p, i, chip_offset, block, gather, total, between):
             base = (chip + chip_offset) % chips * CORES
             rows = [block_rows((base + c) * (chunk // size) + block, size) for c in (1 - core, core)]
             loads = [
                 pltpu.make_async_copy(h_ref.at[row], h_v.at[pl.ds(n * size, size)], h_sem.at[n])
                 for n, row in enumerate(rows)
             ]
-            for load in loads:
-                load.start()
-
             def one_head(head):
-                pl.when(head == heads - 1)(late)
+                @pl.when(head == heads - 2)
+                def _():
+                    gather()
+                    for load in loads:
+                        load.start()
+
+                pl.when(head == heads - 1)(total)
                 attend_head(size, rows, head)
 
             each(heads, one_head)
@@ -398,8 +420,6 @@
                 away[pl.ds(0, size), cols] = both[:size]
                 acc[p % 2, pl.ds(0, size), cols] = both[size:]
                 to_partner(p, i, size, n).start()
-                if n == 0:
-                    flush()
 
         def first_collect(s):
             collect(s, s, FIRST)
@@ -415,15 +435,26 @@
             to_side(s, 1).start()
 
         def first_step(s):
-            @pl.when(s == firsts // 4)
-            def _():
-                for g in range(groups - HELD, groups):
-                    compute_up(jnp.int32(g))
-
-            def late():
+            held = s - firsts // 4
+            has_held = (held >= 0) & (held < HELD)
+
+            @pl.when(has_held)
+            def _():
+                compute_up(groups - HELD + held)
+
+            def gather():
+                @pl.when(has_held)
+                def _():
+                    wait_out(groups - HELD + held)
+
                 @pl.when(s > 0)
                 def _():
                     first_collect(s - 1)
+
+            def total():
+                @pl.when(s > 0)
+                def _():
+                    first_sum(s - 1)
 
             def between():
                 @pl.when(s == 0)
@@ -431,22 +462,12 @@
                     load_wo.wait()
                     load_w2.wait()
 
-                @pl.when(s == firsts // 4)
-                def _():
-                    for g in range(groups - HELD, groups):
-                        wait_out(jnp.int32(g))
-
                 @pl.when(s > 0)
                 def _():
                     sent(s - 1, s - 1, FIRST)
-                    first_sum(s - 1)
-
-            def flush():
-                @pl.when(s > 0)
-                def _():
                     first_send(s - 1)
 
-            partial(FIRST, s, s, 2, s, late, between, flush)
+            partial(FIRST, s, s, 2, s, gather, total, between)
 
         skip = firsts * FIRST // BLOCK
 
@@ -519,7 +540,7 @@
             is_mid, side, block = later_parts(q)
             p = firsts + q
 
-            def late():
+            def gather():
                 @pl.when(q == 0)
                 def _():
                     first_collect(jnp.int32(firsts - 1))
@@ -527,28 +548,28 @@
                 @pl.when(q > 0)
                 def _():
                     later_collect(q - 1)
+
+            def total():
+                @pl.when(q == 0)
+                def _():
+                    first_sum(jnp.int32(firsts - 1))
+
+                @pl.when(q > 0)
+                def _():
+                    later_sum(q - 1)
 
             def between():
                 @pl.when(q == 0)
                 def _():
                     sent(firsts - 1, firsts - 1, FIRST)
-                    first_sum(jnp.int32(firsts - 1))
+                    first_send(jnp.int32(firsts - 1))
 
                 @pl.when(q > 0)
                 def _():
                     sent(p - 1, skip + q - 1, BLOCK)
-                    later_sum(q - 1)
-
-            def flush():
-                @pl.when(q == 0)
-                def _():
-                    first_send(jnp.int32(firsts - 1))
-
-                @pl.when(q > 0)
-                def _():
                     later_send(q - 1)
 
-            partial(BLOCK, p, skip + q, jnp.where(is_mid, 1 + 2 * side, 0), block, late, between, flush)
+            partial(BLOCK, p, skip + q, jnp.where(is_mid, 1 + 2 * side, 0), block, gather, total, between)
 
         later = blocks * (chips - 1)
         each(firsts, first_step)

time: 450 us -> 443 us (0.984)
  Pallas kernels: 444 us -> 437 us
    pallas_call x1, Pallas kernels: 444 us -> 437 us  [transformer_block(): pl.pallas_call(functools.partial(block_kernel, chips), in_specs=[ANY] * 6...]
where the time goes in v5:
time: 443 us; the launch traced here: 442 us
  Pallas kernels  437 us (99%)
  local copies, waits for them, and re-layouts  4.7 us (1%)
    pallas_call x1, Pallas kernels, transformer_block(): pl.pallas_call(functools.partial(block_kernel, chips), in_specs=[ANY] * 6...  437 us

profile of v5, /device:TPU:112, one launch (start us, length us, event | category | flops | bytes accessed | tf_op | source)
XLA Modules:
  0.0 441.9 jit_solution(6154933186621355399)
XLA Ops:
  0.0 437.2 %transformer_block.1 = (bf16[512,4096]{1,0:T(8,128)(2,1)}, bf16[4096,4096]{1,0:T(8,128)(2,1)}, bf16[4096,1376]{1,0:T(8,128)(2,1)}, f32[2048,4096]{1,0:T(8,128)},...) custom-call(bf16[512,4096]{1,0:T(8,128)(2,1)} %x_ref.1, f32[1,4096]{1,0:T(1,128)} %bitcast.5, ...), custom_call_target="tpu_custom_call" | custom-call | tf_op jit(solution)/shard_map/transformer_block/pallas_call | solution.py:620
  437.2 4.7 %copy.8 = bf16[512,4096]{1,0:T(8,128)(2,1)} copy(bf16[512,4096]{1,0:T(8,128)(2,1)} %get-tuple-element.6) | data formatting | bytes 8388608

commit v6 on v5

--- a/solution.py
+++ b/solution.py
@@ -17,6 +17,7 @@
 FIRST = 64
 HELD = 2
 REPACK = 256
+DIRECT = 4
 LATE = 4
 COLS = 2048
 LANES = 512
@@ -342,7 +343,7 @@
             return remote(src, dst, send_o.at[side, b], recv_o.at[side, b], left if side else right)
 
         def to_owner(q, k):
-            side, block = q % 2, q // 2
+            side, block = (q + core) % 2, q // 2
             i = block * slices + k
             src = ps_ref.at[block_rows(firsts * FIRST // PIECE + q * slices + k, PIECE)]
             dst = rn_ref.at[block_rows(side * blocks * slices + i, PIECE)]
@@ -390,9 +391,9 @@
             to_partner(p, i, size, 0).wait_send()
             to_partner(p, i, size, 1).wait_send()
 
-        def partial(size, p, i, chip_offset, block, gather, total, between):
-            base = (chip + chip_offset) % chips * CORES
-            rows = [block_rows((base + c) * (chunk // size) + block, size) for c in (1 - core, core)]
+        def partial(size, p, i, offsets, block, gather, total, between):
+            devices = [(chip + offset) % chips * CORES + c for offset, c in zip(offsets, (1 - core, core))]
+            rows = [block_rows(device * (chunk // size) + block, size) for device in devices]
             loads = [
                 pltpu.make_async_copy(h_ref.at[row], h_v.at[pl.ds(n * size, size)], h_sem.at[n])
                 for n, row in enumerate(rows)
@@ -424,15 +425,30 @@
         def first_collect(s):
             collect(s, s, FIRST)
 
+        def opening_sum(s, side):
+            src = acc.at[s % 2, pl.ds(0, FIRST), pl.ds(side * cols_half, cols_half)]
+            dst = ro_ref.at[block_rows(side * firsts + s, FIRST)]
+            return remote(src, dst, send_o.at[side, s], recv_o.at[side, s], left if side else right)
+
         def first_sum(s):
             stage_partner(s, FIRST).wait()
             add(FIRST, s % 2, 0, stage)
-            spill(s % 2, s, FIRST).start()
+
+            @pl.when(s < DIRECT)
+            def _():
+                opening_sum(s, 0).start()
+                opening_sum(s, 1).start()
+
+            @pl.when(s >= DIRECT)
+            def _():
+                spill(s % 2, s, FIRST).start()
 
         def first_send(s):
-            spill(s % 2, s, FIRST).wait()
-            to_side(s, 0).start()
-            to_side(s, 1).start()
+            @pl.when(s >= DIRECT)
+            def _():
+                spill(s % 2, s, FIRST).wait()
+                to_side(s, 0).start()
+                to_side(s, 1).start()
 
         def first_step(s):
             held = s - firsts // 4
@@ -467,13 +483,18 @@
                     sent(s - 1, s - 1, FIRST)
                     first_send(s - 1)
 
-            partial(FIRST, s, s, 2, s, gather, total, between)
+                @pl.when((s >= 2) & (s < DIRECT + 2))
+                def _():
+                    opening_sum(s - 2, 0).wait_send()
+                    opening_sum(s - 2, 1).wait_send()
+
+            partial(FIRST, s, s, (2, 2), s, gather, total, between)
 
         skip = firsts * FIRST // BLOCK
 
         def later_parts(q):
             is_mid = q < 2 * blocks
-            return is_mid, q % 2, jnp.where(is_mid, q // 2, q - 2 * blocks)
+            return is_mid, (q + core) % 2, jnp.where(is_mid, q // 2, q - 2 * blocks)
 
         def later_collect(q):
             is_mid, side, block = later_parts(q)
@@ -497,43 +518,43 @@
             def _():
                 stage_side(side, block).wait()
                 add(BLOCK, slot, side * cols_half, stage_half)
-                spill(slot, skip + q, BLOCK).start()
-
-            @pl.when(jnp.logical_not(is_mid))
-            def _():
-                def final(k):
-                    i = block * slices + k
-                    rows = block_rows(i, PIECE)
-                    load = pltpu.make_async_copy(x_ref.at[rows], x_v, xr_sem)
-                    load.start()
-                    copies = []
-                    for sd in range(2):
-                        src, sem = rn_ref.at[block_rows(sd * blocks * slices + i, PIECE)], recv_n.at[sd, i]
-                        remote(src, src, sem, sem, partner).wait_recv()
-                        copy = pltpu.make_async_copy(src, stage.at[pl.ds(sd * PIECE, PIECE)], st_sem.at[sd])
-                        copy.start()
-                        copies.append(copy)
-                    load.wait()
-                    for copy in copies:
-                        copy.wait()
-
-                    def tile(n):
-                        cols = pl.ds(pl.multiple_of(n * LANES, LANES), LANES)
-                        mine = acc[slot, block_rows(k, PIECE), cols]
-                        summed = mine + stage[0:PIECE, cols] + stage[PIECE:2 * PIECE, cols]
-                        y_v[:, cols] = (x_v[:, cols].astype(f32) + summed).astype(bf16)
-
-                    each(width // LANES, tile)
-                    store = pltpu.make_async_copy(y_v, y_ref.at[rows], y_sem)
-                    store.start()
-                    store.wait()
-
-                each(slices, final)
+
+            spill(slot, skip + q, BLOCK).start()
+
+        def final(i):
+            rows = block_rows(i, PIECE)
+            load = pltpu.make_async_copy(x_ref.at[rows], x_v, xr_sem)
+            load.start()
+            first_own = (skip + 2 * blocks) * slices
+            own = pltpu.make_async_copy(ps_ref.at[block_rows(first_own + i, PIECE)], acc.at[0, pl.ds(0, PIECE)], ps_sem)
+            own.start()
+            copies = []
+            for sd in range(2):
+                src, sem = rn_ref.at[block_rows(sd * blocks * slices + i, PIECE)], recv_n.at[sd, i]
+                remote(src, src, sem, sem, partner).wait_recv()
+                copy = pltpu.make_async_copy(src, stage.at[pl.ds(sd * PIECE, PIECE)], st_sem.at[sd])
+                copy.start()
+                copies.append(copy)
+            load.wait()
+            own.wait()
+            for copy in copies:
+                copy.wait()
+
+            def tile(n):
+                cols = pl.ds(pl.multiple_of(n * LANES, LANES), LANES)
+                summed = acc[0, 0:PIECE, cols] + stage[0:PIECE, cols] + stage[PIECE:2 * PIECE, cols]
+                y_v[:, cols] = (x_v[:, cols].astype(f32) + summed).astype(bf16)
+
+            each(width // LANES, tile)
+            store = pltpu.make_async_copy(y_v, y_ref.at[rows], y_sem)
+            store.start()
+            store.wait()
 
         def later_send(q):
+            spill((firsts + q) % 2, skip + q, BLOCK).wait()
+
             @pl.when(later_parts(q)[0])
             def _():
-                spill((firsts + q) % 2, skip + q, BLOCK).wait()
                 each(slices, lambda k: to_owner(q, k).start())
 
         def later_step(q):
@@ -569,20 +590,25 @@
                     sent(p - 1, skip + q - 1, BLOCK)
                     later_send(q - 1)
 
-            partial(BLOCK, p, skip + q, jnp.where(is_mid, 1 + 2 * side, 0), block, gather, total, between)
+            offsets = [jnp.where(is_mid, 1 + 2 * sd, 0) for sd in (1 - side, side)]
+            partial(BLOCK, p, skip + q, offsets, block, gather, total, between)
 
         later = blocks * (chips - 1)
         each(firsts, first_step)
         each(later, later_step)
+
+        def finish_side(b):
+            to_side(b + DIRECT, 0).wait_send()
+            to_side(b + DIRECT, 1).wait_send()
+
+        finish_gather()
+        each(firsts - DIRECT, finish_side)
         later_collect(jnp.int32(later - 1))
         later_sum(jnp.int32(later - 1))
+        later_send(jnp.int32(later - 1))
+        each(blocks * slices, final)
         sent(jnp.int32(firsts + later - 1), jnp.int32(skip + later - 1), BLOCK)
 
-        def finish_side(b):
-            to_side(b, 0).wait_send()
-            to_side(b, 1).wait_send()
-
-        each(firsts, finish_side)
         each(2 * blocks, lambda q: each(slices, lambda k: to_owner(q, k).wait_send()))
 
     pl.run_scoped(
@@ -602,7 +628,6 @@
         pltpu.VMEM((PIECE, width), bf16),
         pltpu.VMEM((PIECE, width), bf16),
     )
-    finish_gather()
 
 
 def transformer_block(chips, x_loc, ln_gamma, w_qkv, w_out, w_up_t, w_down):
@@ -628,7 +653,7 @@
             jax.ShapeDtypeStruct((chips * chunk, width), f32),
             jax.ShapeDtypeStruct((2 * chunk, width // 2), f32),
             jax.ShapeDtypeStruct((2 * chunk, width), f32),
-            jax.ShapeDtypeStruct((3 * chunk, width), f32),
+            jax.ShapeDtypeStruct((chips * chunk, width), f32),
         ],
         scratch_shapes=[
             pltpu.VMEM((tokens, heads * qkv_head), bf16),

time: 443 us -> 441 us (level)
  no operation moved by 1% of the time
where the time goes in v6:
time: 441 us; the launch traced here: 439 us
  Pallas kernels  435 us (99%)
  local copies, waits for them, and re-layouts  4.7 us (1%)
    pallas_call x1, Pallas kernels, transformer_block(): pl.pallas_call(functools.partial(block_kernel, chips), in_specs=[ANY] * 6...  435 us

profile of v6, /device:TPU:112, one launch (start us, length us, event | category | flops | bytes accessed | tf_op | source)
XLA Modules:
  0.0 439.3 jit_solution(16128686681193623329)
XLA Ops:
  0.0 434.6 %transformer_block.1 = (bf16[512,4096]{1,0:T(8,128)(2,1)}, bf16[4096,4096]{1,0:T(8,128)(2,1)}, bf16[4096,1376]{1,0:T(8,128)(2,1)}, f32[2048,4096]{1,0:T(8,128)},...) custom-call(bf16[512,4096]{1,0:T(8,128)(2,1)} %x_ref.1, f32[1,4096]{1,0:T(1,128)} %bitcast.5, ...), custom_call_target="tpu_custom_call" | custom-call | tf_op jit(solution)/shard_map/transformer_block/pallas_call | solution.py:645
  434.6 4.7 %copy.8 = bf16[512,4096]{1,0:T(8,128)(2,1)} copy(bf16[512,4096]{1,0:T(8,128)(2,1)} %get-tuple-element.6) | data formatting | bytes 8388608
